TPU v7x, 32 devices: a whole 2x2x4 slice. The times are simulated.
32 devices in a mesh: gx: 4 (over z), gy: 8 (over y, x, core).
Axes of the slice: x: 2, y: 2, z: 4, core: 2. Of those that a mesh axis runs over, the one named last changes fastest.
Arguments:
- populations: float32 [19, 64, 32, 128], P(None, 'gx', 'gy'), as said below
- vert_base: int32 [3, 16384], P(None, ('gx', 'gy')), may hold values from 0 to 127, as said below
- vert_frac: float32 [3, 16384], P(None, ('gx', 'gy')), may hold values from 0 to 0.999
- edges: int32 [2, 49152], P(None, ('gx', 'gy')), may hold values from 0 to 511, as said below
- stiffness: float32 [49152], P(('gx', 'gy')), may hold values from 0.05 to 0.5
- rest: float32 [3, 49152], P(None, ('gx', 'gy')), may hold values from -3 to 3
Outputs:
- fresh: float32 [19, 64, 32, 128], P(None, 'gx', 'gy')
- vertex_velocity: float32 [3, 16384], P(None, ('gx', 'gy'))
Inputs may be any that keep to these rules, and one draw needn't show every extreme that they name: `vert_base`: the first coordinate lies below 64, the second below 32, the third below 128. The vertices are in blocks of 512, block k belonging to the k-th device in the order gx then gy; a vertex's first coordinate lies in that device's 16 cells along x, its second in its 4 cells along y. Each run of 128 vertices of a block lies in a box of 4 x 4 x 4 cells, periodic in z. `edges`: edge e belongs to block e // 1536; its two entries are distinct indices within that block's 512 vertices, both in the same run of 128 vertices. `populations`: every entry lies between 0.6 and 1.4 times the lattice weight of its direction.
All inputs are finite; a program needn't handle non-finite values.
Results may differ from a plain program's by a relative error of at most 0.000078.
Values sent between devices are 32-bit elements; how exact they have to be, the bound alone decides.
A program may use at most 64 MiB of HBM per device.

v0:
```python
import jax
import jax.numpy as jnp
from jax import lax
from jax.experimental import pallas as pl
from jax.experimental.pallas import tpu as pltpu
from jax.sharding import PartitionSpec as P

lattice_speeds = [
    (0, 0, 0),
    (1, 0, 0),
    (-1, 0, 0),
    (0, 1, 0),
    (0, -1, 0),
    (0, 0, 1),
    (0, 0, -1),
    (1, 1, 0),
    (-1, -1, 0),
    (1, -1, 0),
    (-1, 1, 0),
    (1, 0, 1),
    (-1, 0, -1),
    (1, 0, -1),
    (-1, 0, 1),
    (0, 1, 1),
    (0, -1, -1),
    (0, 1, -1),
    (0, -1, 1),
]
lattice_weights = [1.0 / 3.0] + [1.0 / 18.0] * 6 + [1.0 / 36.0] * 12
relax_time = 0.9
run = 128
sides = [(1, 1), (1, -1), (-1, 1), (-1, -1), (0, 1), (0, -1), (1, 0), (-1, 0)]
f32, bf16 = jnp.float32, jnp.bfloat16


def outer_weight(r):
    return (5.0 - 2.0 * r - jnp.sqrt(-7.0 + 12.0 * r - 4.0 * r * r)) / 8.0


def inner_weight(r):
    return (3.0 - 2.0 * r + jnp.sqrt(1.0 + 4.0 * r - 4.0 * r * r)) / 8.0


def up8(n):
    return (n + 7) // 8 * 8


class Plan:
    def __init__(self, wx, wy):
        self.wx, self.wy = wx, wy
        self.own = wx * wy
        self.xh = self.own
        self.yh = self.xh + 4 * wy
        self.co = self.yh + 3 * wx
        self.rows = self.co + 16
        hx, hy = [-1, wx, wx + 1], [-1, wy, wy + 1]
        self.row = {}
        for x in range(wx):
            for y in range(wy):
                self.row[x, y] = x * wy + y
        for k in range(3):
            for y in range(wy):
                self.row[hx[k], y] = self.xh + k * wy + y
            for x in range(wx):
                self.row[x, hy[k]] = self.yh + k * wx + x
            for m in range(3):
                self.row[hx[m], hy[k]] = self.co + 3 * k + m
        self.pads = [(self.xh + 3 * wy, wy), (self.co + 9, 7)]

        def span(d, w):
            full = list(range(w)) + [-1, w, w + 1]
            return {0: full, 1: [w - 1, w, w + 1], -1: [-1, 0, 1]}[d]

        def edge(d, w):
            return {0: list(range(w)), 1: [w - 1], -1: [0, 1]}[d]

        def near(d, w):
            return {0: list(range(w)), 1: [w - 1], -1: [0]}[d]

        def cells(d, pick):
            xs, ys = pick(d[0], wx), pick(d[1], wy)
            if d[1]:
                return [(x, y) for y in ys for x in xs]
            return [(x, y) for x in xs for y in ys]

        self.force = [cells(d, span) for d in sides]
        self.edge = [cells(d, edge) for d in sides]
        self.near = [cells(d, near) for d in sides]
        self.dirs = [
            [
                q
                for q, c in enumerate(lattice_speeds)
                if (not d[0] or c[0] == d[0]) and (not d[1] or c[1] == d[1])
            ]
            for d in sides
        ]
        self.force_rows = [up8(3 * len(c)) for c in self.force]
        self.macro_rows = [
            up8(4 * len(e) + len(q) * len(n)) for e, q, n in zip(self.edge, self.dirs, self.near)
        ]

    def there(self, cell, d):
        return self.row[cell[0] - d[0] * self.wx, cell[1] - d[1] * self.wy]


def runs(src, dst):
    out, i = [], 0
    while i < len(src):
        n, a, b = 1, 1, 1
        if i + 1 < len(src) and src[i + 1] > src[i] and dst[i + 1] > dst[i]:
            a, b = src[i + 1] - src[i], dst[i + 1] - dst[i]
            n = 2
            while i + n < len(src) and src[i + n] - src[i + n - 1] == a and dst[i + n] - dst[i + n - 1] == b:
                n += 1
        out.append((src[i], a, dst[i], b, n))
        i += n
    return out


def ds(start, n, stride):
    return pl.ds(start, n, stride=stride) if stride > 1 else pl.ds(start, n)


def move(src_ref, src, dst_ref, dst, add=False):
    for s, a, d, b, n in runs(src, dst):
        value = src_ref[ds(s, n, a), :]
        if add:
            value = value + dst_ref[ds(d, n, b), :]
        dst_ref[ds(d, n, b), :] = value


def split(value):
    high = value.astype(bf16)
    return high, (value - high.astype(f32)).astype(bf16)


def pick4(delta, weights):
    out = jnp.zeros(delta.shape, f32)
    for k in range(4):
        out = jnp.where(delta == k, weights[k], out)
    return out


def exchange_kernel(plan, nx, ny, *refs):
    wx, wy, rows, own = plan.wx, plan.wy, plan.rows, plan.own
    sources, results, scratch = refs[0:6], refs[6:12], refs[12:]
    pops, ext, grid, halo, plane, along = results
    ms, mr, fs, fr = scratch[0:8], scratch[8:16], scratch[16:24], scratch[24:32]
    base, frac, edges, stiff, rest, pos, pull, mem, sems, load_sems = scratch[32:]
    targets = (pops, base, frac, edges, stiff, rest)
    loads_in = [pltpu.make_async_copy(sources[n], targets[n], load_sems.at[n]) for n in range(6)]
    for n in (3, 2, 1, 5, 4, 0):
        loads_in[n].start()
    count, depth = base.shape[1], pops.shape[1]
    edge_count = edges.shape[1]
    tiles = count // run
    ix, iy = lax.axis_index("gx"), lax.axis_index("gy")
    peers = [(lax.rem(ix + dx + nx, nx), lax.rem(iy + dy + ny, ny)) for dx, dy in sides]
    barrier = pltpu.get_barrier_semaphore()
    for peer in peers:
        pl.semaphore_signal(barrier, inc=1, device_id=peer, device_id_type=pl.DeviceIdType.MESH)

    def copies(src, dst, kind):
        return [
            pltpu.make_async_remote_copy(
                src_ref=src[n],
                dst_ref=dst[n],
                send_sem=sems.at[kind, n],
                recv_sem=sems.at[kind + 1, n],
                device_id=peers[n],
                device_id_type=pl.DeviceIdType.MESH,
            )
            for n in range(8)
        ]

    macro_copies = copies(ms, mr, 0)
    force_copies = copies(fs, fr, 2)

    pos[...] = jnp.zeros(pos.shape, f32)
    pull[...] = jnp.zeros(pull.shape, f32)
    for n in (3, 2, 1, 5, 4):
        loads_in[n].wait()
    part = 8 * tiles
    moved = frac[...]
    high = moved.astype(bf16).astype(f32)
    low = moved - high
    whole = base[...].astype(f32)
    for t in range(tiles):
        cols = slice(t * run, (t + 1) * run)
        pos[pl.ds(8 * t, 3), :] = whole[:, cols]
        pos[pl.ds(part + 8 * t, 3), :] = high[:, cols]
        pos[pl.ds(2 * part + 8 * t, 3), :] = low[:, cols]
    ends = edges[...]
    spot = lax.broadcasted_iota(jnp.int32, (run, edge_count), 0)
    tail = jnp.bitwise_and(ends[0:1], run - 1)
    head = jnp.bitwise_and(ends[1:2], run - 1)
    hot = (jnp.where(spot == head, 1.0, 0.0) - jnp.where(spot == tail, 1.0, 0.0)).astype(bf16)
    group = lax.shift_right_logical(ends[0:1], run.bit_length() - 1)
    reach = jnp.dot(pos[...].astype(bf16), hot, preferred_element_type=f32)
    reach = reach[0:part] + reach[part : 2 * part] + reach[2 * part : 3 * part]
    pull[pl.ds(0, 3), :] = rest[...]
    diff = jnp.zeros((8, edge_count), f32)
    for t in range(tiles):
        diff = jnp.where(group == t, reach[8 * t : 8 * t + 8], diff)
    stretch = stiff[...].reshape(1, edge_count) * (diff - pull[...])
    terms = jnp.concatenate([jnp.where(group == t, stretch, 0.0) for t in range(tiles)], axis=0)
    big, small = split(terms)
    both = jnp.concatenate([big, small], axis=0)
    summed = lax.dot_general(both, hot, (((1,), (1,)), ((), ())), preferred_element_type=f32)
    summed = summed[0:part] + summed[part : 2 * part]
    for t in range(tiles):
        mem[:, t * run : (t + 1) * run] = -summed[8 * t : 8 * t + 8]

    weights = [
        outer_weight(1.0 + moved),
        inner_weight(moved),
        inner_weight(1.0 - moved),
        outer_weight(2.0 - moved),
    ]
    bx = base[0:1, :] - ix * wx - 1
    by = base[1:2, :] - iy * wy - 1
    bz = base[2:3, :] - 1
    gap = lax.broadcasted_iota(jnp.int32, (depth, count), 0) - bz
    gap = jnp.where(gap < 0, gap + depth, gap)
    gap = jnp.where(gap >= depth, gap - depth, gap)
    along_z = pick4(gap, [w[2:3] for w in weights])
    z_high, z_low = split(along_z)
    along[pl.ds(0, depth), :] = z_high
    along[pl.ds(depth, depth), :] = z_low
    far = -100
    for r in range(0, rows, 16):
        i = lax.broadcasted_iota(jnp.int32, (16, 1), 0)
        if r < plan.xh:
            i = i + r
            x = i // wy
            y = i - x * wy
        elif r < plan.yh:
            i = i + (r - plan.xh)
            k = i // wy
            x = jnp.where(k == 0, -1, jnp.where(k == 3, far, wx - 1 + k))
            y = i - k * wy
        elif r < plan.co:
            k = (r - plan.yh) // wx
            x = i + (r - plan.yh - k * wx)
            y = jnp.full((16, 1), (-1, wy, wy + 1)[k], jnp.int32)
        else:
            k = jnp.where(i >= 6, 2, jnp.where(i >= 3, 1, 0))
            m = i - 3 * k
            x = jnp.where(m == 0, -1, jnp.where(m >= 3, far, wx - 1 + m))
            y = jnp.where(k == 0, -1, wy - 1 + k)
        px = pick4(x - bx, [w[0:1] for w in weights])
        py = pick4(y - by, [w[1:2] for w in weights])
        plane[pl.ds(r, 16), :] = px * py
    flat = plane[...]
    loads = [split(flat * mem[c : c + 1, :]) for c in range(3)]
    stack = jnp.concatenate([h for h, _ in loads] + [l for _, l in loads], axis=0)
    spread = lax.dot_general(stack, along[...], (((1,), (1,)), ((), ())), preferred_element_type=f32)
    spread = spread[0 : 3 * rows] + spread[3 * rows : 6 * rows]
    grid[...] = spread[:, 0:depth] + spread[:, depth : 2 * depth]
    for n in range(8):
        cells = plan.force[n]
        for k in range(3):
            move(grid, [k * rows + plan.row[c] for c in cells], fs[n], [k * len(cells) + i for i in range(len(cells))])
    loads_in[0].wait()
    for r in range(0, own, 16):
        totals = [None] * 4
        for q, c in enumerate(lattice_speeds):
            value = pops[pl.ds(q * own + r, 16), :]
            for k, sign in enumerate((1,) + c):
                if sign:
                    term = value if sign > 0 else -value
                    totals[k] = term if totals[k] is None else totals[k] + term
        for k in range(4):
            ext[pl.ds(k * rows + r, 16), :] = totals[k]
    for start, n in plan.pads:
        for k in range(4):
            ext[pl.ds(k * rows + start, n), :] = jnp.full((n, depth), 0.0 if k else 1.0, f32)
    for n in range(8):
        cells, close = plan.edge[n], plan.near[n]
        for k in range(4):
            move(ext, [k * rows + plan.row[c] for c in cells], ms[n], [k * len(cells) + i for i in range(len(cells))])
        for s, q in enumerate(plan.dirs[n]):
            first = 4 * len(cells) + s * len(close)
            move(pops, [q * own + plan.row[c] for c in close], ms[n], [first + i for i in range(len(close))])

    pl.semaphore_wait(barrier, 8)
    for copy in macro_copies:
        copy.start()

    for copy in force_copies:
        copy.start()

    for n in range(8):
        macro_copies[n].wait_recv()
        cells, close, d = plan.edge[n], plan.near[n], sides[n]
        for k in range(4):
            move(mr[n], [k * len(cells) + i for i in range(len(cells))], ext, [k * rows + plan.there(c, d) for c in cells])
        for s, q in enumerate(plan.dirs[n]):
            first = 4 * len(cells) + s * len(close)
            move(mr[n], [first + i for i in range(len(close))], halo, [q * rows + plan.there(c, d) for c in close])
    for n in range(8):
        force_copies[n].wait_recv()
        cells, d = plan.force[n], sides[n]
        for k in range(3):
            move(fr[n], [k * len(cells) + i for i in range(len(cells))], grid, [k * rows + plan.there(c, d) for c in cells], add=True)

    for copy in macro_copies + force_copies:
        copy.wait_send()


def collide_kernel(plan, pops, ext, grid, halo, plane, along, fresh_out, sampled_out, *scratch):
    wx, wy, rows, own = plan.wx, plan.wy, plan.rows, plan.own
    fresh, sampled, post, vel, sems = scratch
    depth = pops.shape[1]
    leave = [
        pltpu.make_async_copy(
            fresh.at[pl.ds(q * own, own), :], fresh_out.at[pl.ds(q * own, own), :], sems.at[q]
        )
        for q in range(19)
    ]
    leave.append(pltpu.make_async_copy(sampled, sampled_out, sems.at[19]))
    keep = 1.0 - 1.0 / relax_time
    half = 1.0 - 0.5 / relax_time

    def along_speed(c, vector):
        total = None
        for k in range(3):
            if c[k]:
                term = vector[k] if c[k] > 0 else -vector[k]
                total = term if total is None else total + term
        return total

    for r in range(0, rows, 16):
        density = ext[pl.ds(r, 16), :]
        force = [grid[pl.ds(k * rows + r, 16), :] for k in range(3)]
        inverse = 1.0 / density
        speed = [(ext[pl.ds((k + 1) * rows + r, 16), :] + 0.5 * force[k]) * inverse for k in range(3)]
        for k in range(3):
            vel[pl.ds(k * rows + r, 16), :] = speed[k]
        if r < own:
            need = list(range(19))
        elif r < plan.yh:
            need = [q for q in range(19) if lattice_speeds[q][0]]
        elif r < plan.yh + wx:
            need = [q for q in range(19) if lattice_speeds[q][1] == 1]
        elif r < plan.yh + 2 * wx:
            need = [q for q in range(19) if lattice_speeds[q][1] == -1]
        elif r < plan.co:
            continue
        else:
            need = [q for q in range(19) if lattice_speeds[q][0] and lattice_speeds[q][1]]
        square = speed[0] * speed[0] + speed[1] * speed[1] + speed[2] * speed[2]
        work = speed[0] * force[0] + speed[1] * force[1] + speed[2] * force[2]
        scaled = density * (1.0 / relax_time)
        level = scaled * (1.0 - 1.5 * square) - (3.0 * half) * work
        for first in [0] + list(range(1, 19, 2)):
            pair = [0] if first == 0 else [first, first + 1]
            if not any(q in need for q in pair):
                continue
            weight = lattice_weights[first]
            if first == 0:
                even, odd = level * weight, None
            else:
                a = along_speed(lattice_speeds[first], speed)
                push = along_speed(lattice_speeds[first], force)
                turn = scaled * a + half * push
                even = weight * (level + a * (4.5 * scaled * a + 9.0 * half * push))
                odd = (3.0 * weight) * turn
            for q in pair:
                if q not in need:
                    continue
                c = lattice_speeds[q]
                if r < own:
                    value = pops[pl.ds(q * own + r, 16), :]
                else:
                    value = halo[pl.ds(q * rows + r, 16), :]
                value = keep * value + even
                if odd is not None:
                    value = value + odd if q == first else value - odd
                if c[2]:
                    value = pltpu.roll(value, c[2] % depth, 1)
                if c[0] == 0 and c[1] == 0:
                    fresh[pl.ds(q * own + r, 16), :] = value
                else:
                    post[pl.ds(q * rows + r, 16), :] = value
    for q, c in enumerate(lattice_speeds):
        if c[0] == 0 and c[1] == 0:
            leave[q].start()
            continue
        if c[1]:
            cells = [(x, y) for y in range(wy) for x in range(wx)]
        else:
            cells = [(x, y) for x in range(wx) for y in range(wy)]
        move(
            post,
            [q * rows + plan.row[x - c[0], y - c[1]] for x, y in cells],
            fresh,
            [q * own + x * wy + y for x, y in cells],
        )
        leave[q].start()

    v_high, v_low = split(vel[...])
    value = jnp.dot(v_high, along[pl.ds(0, depth), :], preferred_element_type=f32)
    value = value + jnp.dot(v_low, along[pl.ds(0, depth), :], preferred_element_type=f32)
    value = value + jnp.dot(v_high, along[pl.ds(depth, depth), :], preferred_element_type=f32)
    flat = plane[...]
    for k in range(3):
        sampled[k : k + 1, :] = jnp.sum(value[k * rows : (k + 1) * rows] * flat, axis=0, keepdims=True)
    leave[19].start()
    for copy in leave:
        copy.wait()


def solution(mesh):
    nx, ny = mesh.shape["gx"], mesh.shape["gy"]

    def per_device(populations, vert_base, vert_frac, edges, stiffness, rest):
        _, wx, wy, depth = populations.shape
        count, edge_count = vert_base.shape[1], edges.shape[1]
        plan = Plan(wx, wy)
        rows, tiles = plan.rows, count // run
        macro = [pltpu.VMEM((n, depth), f32) for n in plan.macro_rows]
        force = [pltpu.VMEM((n, depth), f32) for n in plan.force_rows]
        scratch = macro + macro + force + force
        scratch += [
            pltpu.VMEM((3, count), jnp.int32),
            pltpu.VMEM((3, count), f32),
            pltpu.VMEM((2, edge_count), jnp.int32),
            pltpu.VMEM((edge_count,), f32),
            pltpu.VMEM((3, edge_count), f32),
            pltpu.VMEM((24 * tiles, run), f32),
            pltpu.VMEM((8, edge_count), f32),
            pltpu.VMEM((8, count), f32),
            pltpu.SemaphoreType.DMA((4, 8)),
            pltpu.SemaphoreType.DMA((6,)),
        ]
        vmem = pl.BlockSpec(memory_space=pltpu.VMEM)
        far = pl.BlockSpec(memory_space=pltpu.HBM)

        def exchange(*refs):
            exchange_kernel(plan, nx, ny, *refs)

        def collide(*refs):
            collide_kernel(plan, *refs)

        held = pl.pallas_call(
            exchange,
            out_shape=(
                jax.ShapeDtypeStruct((19 * wx * wy, depth), f32),
                jax.ShapeDtypeStruct((4 * rows, depth), f32),
                jax.ShapeDtypeStruct((3 * rows, depth), f32),
                jax.ShapeDtypeStruct((19 * rows, depth), f32),
                jax.ShapeDtypeStruct((rows, count), f32),
                jax.ShapeDtypeStruct((2 * depth, count), bf16),
            ),
            in_specs=[far] * 6,
            out_specs=(vmem,) * 6,
            scratch_shapes=scratch,
            compiler_params=pltpu.CompilerParams(
                collective_id=0, has_side_effects=True, vmem_limit_bytes=24 * 1024 * 1024
            ),
            name="exchange",
        )(
            *[
                pltpu.with_memory_space_constraint(value, pltpu.HBM)
                for value in (
                    populations.reshape(19 * wx * wy, depth),
                    vert_base,
                    vert_frac,
                    edges,
                    stiffness,
                    rest,
                )
            ]
        )
        fresh, sampled = pl.pallas_call(
            collide,
            out_shape=(
                jax.ShapeDtypeStruct((19 * wx * wy, depth), f32),
                jax.ShapeDtypeStruct((3, count), f32),
            ),
            in_specs=[vmem] * 6,
            out_specs=(far, far),
            scratch_shapes=[
                pltpu.VMEM((19 * wx * wy, depth), f32),
                pltpu.VMEM((3, count), f32),
                pltpu.VMEM((19 * rows, depth), f32),
                pltpu.VMEM((3 * rows, depth), f32),
                pltpu.SemaphoreType.DMA((20,)),
            ],
            compiler_params=pltpu.CompilerParams(vmem_limit_bytes=24 * 1024 * 1024),
            name="collide",
        )(*held)
        return fresh.reshape(19, wx, wy, depth), sampled

    placed = (
        P(None, "gx", "gy", None),
        P(None, ("gx", "gy")),
        P(None, ("gx", "gy")),
        P(None, ("gx", "gy")),
        P(("gx", "gy")),
        P(None, ("gx", "gy")),
    )
    return jax.shard_map(
        per_device,
        mesh=mesh,
        in_specs=placed,
        out_specs=(P(None, "gx", "gy", None), P(None, ("gx", "gy"))),
        check_vma=False,
    )
```

profile of v0, /device:TPU:0, one launch (start us, length us, event | category | flops | bytes accessed | tf_op | source)
XLA Modules:
  0.0 14.7 jit_solution(2360430269210437932)
XLA Ops:
  0.6 12.6 %exchange.1 = (f32[1216,128]{1,0:T(8,128)S(1)}, f32[576,128]{1,0:T(8,128)S(1)}, f32[432,128]{1,0:T(8,128)S(1)}, f32[2736,128]{1,0:T(8,128)S(1)}, f32[144,512]{1,0:T(8,128)S(1)}, /*index=5*/bf16[256,512]{1,0:T(8,128)(2,1)S(1)}) custom-call(f32[1216,128]{1,0:T(8,128)} %bitcast.2, s32[3,512]{1,0:T(4,128)} %refs_1_.1, f32[3,512]{1,0:T(4,128)} %refs_2_.1, ...), custom_call_target="tpu_custom_call" | custom-call | tf_op jit(solution)/shard_map/exchange/pallas_call | solution.py:446
  13.2 1.4 %collide.1 = (f32[1216,128]{1,0:T(8,128)}, f32[3,512]{1,0:T(4,128)}) custom-call(f32[1216,128]{1,0:T(8,128)S(1)} %get-tuple-element.10.refs_0_, f32[576,128]{1,0:T(8,128)S(1)} %get-tuple-element.11.refs_1_, f32[432,128]{1,0:T(8,128)S(1)} %get-tuple-element.12.refs_2_, f32[2736,128]{1,0:T(8,128)S(1)} %get-tuple-element.13.refs_3_, ...), custom_call_target="tpu_custom_call" | custom-call | tf_op jit(solution)/shard_map/collide/pallas_call | solution.py:476
where the time goes:
time: 14.9 us; the launch traced here: 14.7 us
  Pallas kernels  14 us (94%)
  between operations  0.64 us (4%)
    pallas_call x1, Pallas kernels, per_device(): pl.pallas_call(exchange, out_shape=(jax.ShapeDtypeStruct((19 * wx * wy, d...  12.6 us
    pallas_call x1, Pallas kernels, per_device(): pl.pallas_call(collide, out_shape=(jax.ShapeDtypeStruct((19 * wx * wy, de...  1.43 us

commit v1 on v0

v1 whole, which is shorter than its diff:
```python
import jax
import jax.numpy as jnp
from jax import lax
from jax.experimental import pallas as pl
from jax.experimental.pallas import tpu as pltpu
from jax.sharding import PartitionSpec as P

lattice_speeds = [
    (0, 0, 0),
    (1, 0, 0),
    (-1, 0, 0),
    (0, 1, 0),
    (0, -1, 0),
    (0, 0, 1),
    (0, 0, -1),
    (1, 1, 0),
    (-1, -1, 0),
    (1, -1, 0),
    (-1, 1, 0),
    (1, 0, 1),
    (-1, 0, -1),
    (1, 0, -1),
    (-1, 0, 1),
    (0, 1, 1),
    (0, -1, -1),
    (0, 1, -1),
    (0, -1, 1),
]
lattice_weights = [1.0 / 3.0] + [1.0 / 18.0] * 6 + [1.0 / 36.0] * 12
relax_time = 0.9
run = 128
window = 8
sides = [(1, 1), (1, -1), (-1, 1), (-1, -1), (0, 1), (0, -1), (1, 0), (-1, 0)]
groups = [(0, 1, 6), (2, 3, 7), (4,), (5,)]
f32, bf16 = jnp.float32, jnp.bfloat16


def outer_weight(r):
    return (5.0 - 2.0 * r - jnp.sqrt(-7.0 + 12.0 * r - 4.0 * r * r)) / 8.0


def inner_weight(r):
    return (3.0 - 2.0 * r + jnp.sqrt(1.0 + 4.0 * r - 4.0 * r * r)) / 8.0


def up(n, m):
    return (n + m - 1) // m * m


class Plan:
    def __init__(self, wx, wy):
        self.wx, self.wy, self.own = wx, wy, wx * wy
        self.h = up(wy + 3, 8)
        self.cols = wx + 3
        self.rows = up(self.cols * self.h, 16)
        self.xs = list(range(-1, wx + 2))

        def span(d, w):
            return {0: list(range(-1, w + 2)), 1: [w - 1, w, w + 1], -1: [-1, 0, 1]}[d]

        def edge(d, w):
            return {0: list(range(w)), 1: [w - 1], -1: [0, 1]}[d]

        def near(d, w):
            return {0: list(range(w)), 1: [w - 1], -1: [0]}[d]

        def cells(d, pick):
            xs, ys = pick(d[0], wx), pick(d[1], wy)
            if d[0]:
                return [(x, y) for x in xs for y in ys]
            return [(x, y) for y in ys for x in xs]

        self.edge = [cells(d, edge) for d in sides]
        self.near = [cells(d, near) for d in sides]
        self.force = [cells(d, span) for d in sides]
        self.dirs = [
            [
                q
                for q, c in enumerate(lattice_speeds)
                if (not d[0] or c[0] == d[0]) and (not d[1] or c[1] == d[1])
            ]
            for d in sides
        ]
        self.macro_rows = [
            4 * len(e) + len(q) * len(n) + 1 for e, q, n in zip(self.edge, self.dirs, self.near)
        ]
        self.force_rows = [3 * self.h if d[1] == 0 else len(c) for d, c in zip(sides, self.force)]

    def row(self, x, y):
        return (x + 1) * self.h + y % self.h

    def there(self, cell, d):
        return self.row(cell[0] - d[0] * self.wx, cell[1] - d[1] * self.wy)

    def late(self, x):
        return x < 2 or x > self.wx - 2


def runs(src, dst):
    out, i = [], 0
    while i < len(src):
        n, a, b = 1, 1, 1
        if i + 1 < len(src) and src[i + 1] > src[i] and dst[i + 1] > dst[i]:
            a, b = src[i + 1] - src[i], dst[i + 1] - dst[i]
            n = 2
            while i + n < len(src) and src[i + n] - src[i + n - 1] == a and dst[i + n] - dst[i + n - 1] == b:
                n += 1
        out.append((src[i], a, dst[i], b, n))
        i += n
    return out


def ds(start, n, stride):
    return pl.ds(start, n, stride=stride) if stride > 1 else pl.ds(start, n)


def move(src_ref, src, dst_ref, dst):
    for s, a, d, b, n in runs(src, dst):
        dst_ref[ds(d, n, b), :] = src_ref[ds(s, n, a), :]


def split(value):
    high = value.astype(bf16)
    return high, (value - high.astype(f32)).astype(bf16)


def halves(value):
    return jnp.concatenate(split(value), axis=0)


def pick4(delta, weights):
    out = jnp.zeros(delta.shape, f32)
    for k in range(4):
        out = jnp.where(delta == k, weights[k], out)
    return out


def wrap(value, depth):
    value = jnp.where(value < 0, value + depth, value)
    return jnp.where(value >= depth, value - depth, value)


def along_speed(c, vector):
    total = None
    for k in range(3):
        if c[k]:
            term = vector[k] if c[k] > 0 else -vector[k]
            total = term if total is None else total + term
    return total


def transposed_dot(a, b):
    return lax.dot_general(a, b, (((1,), (1,)), ((), ())), preferred_element_type=f32)


def exchange_kernel(plan, nx, ny, *refs):
    wx, wy, h, rows, own = plan.wx, plan.wy, plan.h, plan.rows, plan.own
    sources, results, scratch = refs[0:6], refs[6:10], refs[10:]
    fresh, vel, plane, along = results
    ms, mr, fs, fr = scratch[0:8], scratch[8:16], scratch[16:24], scratch[24:32]
    (pops, base, frac, edges, stiff, rest, pos, pull, mem, mac, grid, comb, px_ref) = scratch[32:45]
    placed = scratch[45:53]
    ones_y, ones_l, ones_r, edge_pops, sems, load_sems, ready = scratch[53:]
    depth = pops.shape[1]
    load_into = (pops.at[pl.ds(0, 19 * own), :], base, frac, edges, stiff, rest)
    loads_in = [pltpu.make_async_copy(sources[n], load_into[n], load_sems.at[n]) for n in range(6)]
    for n in (3, 2, 1, 5, 4, 0):
        loads_in[n].start()
    count = base.shape[1]
    edge_count = edges.shape[1]
    tiles = count // run
    ix, iy = lax.axis_index("gx"), lax.axis_index("gy")
    peers = [(lax.rem(ix + dx + nx, nx), lax.rem(iy + dy + ny, ny)) for dx, dy in sides]
    key = ix * ny + iy
    lead = [(key < peers[g[0]][0] * ny + peers[g[0]][1]).astype(jnp.int32) for g in groups]
    barrier = pltpu.get_barrier_semaphore()

    def hail(sem, n):
        pl.semaphore_signal(sem, inc=1, device_id=peers[n], device_id_type=pl.DeviceIdType.MESH)

    for i, g in enumerate(groups):

        @pl.when(lead[i] == 1)
        def _():
            for n in g:
                hail(barrier, n)

    greetings = sum((1 - lead[i]) * len(g) for i, g in enumerate(groups))

    @pl.when(greetings > 0)
    def _():
        pl.semaphore_wait(barrier, greetings)

    for i, g in enumerate(groups):

        @pl.when(lead[i] == 0)
        def _():
            for n in g:
                hail(ready.at[sides.index((-sides[n][0], -sides[n][1]))], n)

    def copies(src, dst, kind):
        return [
            pltpu.make_async_remote_copy(
                src_ref=src[n],
                dst_ref=dst[n],
                send_sem=sems.at[kind, n],
                recv_sem=sems.at[kind + 1, n],
                device_id=peers[n],
                device_id_type=pl.DeviceIdType.MESH,
            )
            for n in range(8)
        ]

    first_col = {1: wx, -1: 0}
    outgoing = list(fs)
    for n in (6, 7):
        outgoing[n] = comb.at[pl.ds(first_col[sides[n][0]] * h, 3 * h), :]
    macro_copies = copies(ms, mr, 0)
    force_copies = copies(outgoing, fr, 2)

    zeros = jnp.zeros((8, run), f32)
    pos[...] = jnp.zeros(pos.shape, f32)
    pull[...] = jnp.zeros(pull.shape, f32)
    for ref in placed:
        ref[...] = jnp.zeros(ref.shape, f32)
    for n in (3, 2, 1, 5, 4):
        loads_in[n].wait()

    moved = frac[...]
    weights = [
        outer_weight(1.0 + moved),
        inner_weight(moved),
        inner_weight(1.0 - moved),
        outer_weight(2.0 - moved),
    ]
    lane = lax.broadcasted_iota(jnp.int32, (1, run), 1)
    slot = lax.rem(lane, window)
    of_tile = lax.rem(lane // window, tiles)
    start_of = jnp.zeros((1, run), jnp.int32)
    offsets = []
    for t in range(tiles):
        z = base[2:3, t * run : (t + 1) * run]
        gap = z - z[0:1, 0:1]
        gap = jnp.where(gap > depth // 2, gap - depth, gap)
        gap = jnp.where(gap < -(depth // 2), gap + depth, gap)
        low = jnp.min(gap, axis=1, keepdims=True)
        offsets.append(gap - low)
        start_of = jnp.where(of_tile == t, z[0:1, 0:1] + low - 1, start_of)
    zmap = wrap(start_of + slot, depth).astype(f32)
    offset = jnp.concatenate(offsets, axis=1)
    reach_z = pick4(lax.broadcasted_iota(jnp.int32, (window, count), 0) - offset, [w[2:3] for w in weights])

    loads_in[0].wait()
    for r in range(0, own, 8):
        totals = [None] * 4
        for q, c in enumerate(lattice_speeds):
            value = pops[pl.ds(q * own + r, 8), :]
            for k, sign in enumerate((1,) + c):
                if sign:
                    term = value if sign > 0 else -value
                    totals[k] = term if totals[k] is None else totals[k] + term
        for k in range(4):
            for i in range(0, 8, wy):
                mac[pl.ds(k * rows + plan.row((r + i) // wy, 0), wy), :] = totals[k][i : i + wy]
    for n in range(8):
        cells, close = plan.edge[n], plan.near[n]
        for k in range(4):
            move(
                mac,
                [k * rows + plan.row(x, y) for x, y in cells],
                ms[n],
                [k * len(cells) + i for i in range(len(cells))],
            )
        for s, q in enumerate(plan.dirs[n]):
            first = 4 * len(cells) + s * len(close)
            move(pops, [q * own + x * wy + y for x, y in close], ms[n], [first + i for i in range(len(close))])
        ms[n][pl.ds(plan.macro_rows[n] - 1, 1), :] = zmap
    for i, g in enumerate(groups):

        @pl.when(lead[i] == 0)
        def _():
            for n in g:
                macro_copies[n].start()

    part = 8 * tiles
    high = moved.astype(bf16).astype(f32)
    low = moved - high
    whole = base[...].astype(f32)
    for t in range(tiles):
        cols = slice(t * run, (t + 1) * run)
        pos[pl.ds(8 * t, 3), :] = whole[:, cols]
        pos[pl.ds(part + 8 * t, 3), :] = high[:, cols]
        pos[pl.ds(2 * part + 8 * t, 3), :] = low[:, cols]
    ends = edges[...]
    spot = lax.broadcasted_iota(jnp.int32, (run, edge_count), 0)
    tail = jnp.bitwise_and(ends[0:1], run - 1)
    head = jnp.bitwise_and(ends[1:2], run - 1)
    hot = jnp.where(spot == head, 1.0, jnp.where(spot == tail, -1.0, 0.0)).astype(bf16)
    group = lax.shift_right_logical(ends[0:1], run.bit_length() - 1)
    reach = jnp.dot(pos[...].astype(bf16), hot, preferred_element_type=f32)
    reach = reach[0:part] + reach[part : 2 * part] + reach[2 * part : 3 * part]
    pull[pl.ds(0, 3), :] = rest[...]
    diff = jnp.zeros((8, edge_count), f32)
    for t in range(tiles):
        diff = jnp.where(group == t, reach[8 * t : 8 * t + 8], diff)
    stretch = stiff[...].reshape(1, edge_count) * (diff - pull[...])
    terms = jnp.concatenate([jnp.where(group == t, stretch, 0.0) for t in range(tiles)], axis=0)
    summed = transposed_dot(halves(terms), hot)
    summed = summed[0:part] + summed[part : 2 * part]
    for t in range(tiles):
        mem[:, t * run : (t + 1) * run] = -summed[8 * t : 8 * t + 8]

    bx = base[0:1, :] - ix * wx - 1
    by = base[1:2, :] - iy * wy - 1
    i = lax.broadcasted_iota(jnp.int32, (px_ref.shape[0], 1), 0)
    px_ref[...] = pick4(i - 1 - bx, [w[0:1] for w in weights])
    i = lax.broadcasted_iota(jnp.int32, (h, 1), 0)
    y = jnp.where(i == h - 1, -1, jnp.where(i > wy + 1, -100, i))
    py = pick4(y - by, [w[1:2] for w in weights])
    for k in range(rows // h):
        if k < plan.cols:
            plane[pl.ds(k * h, h), :] = px_ref[pl.ds(k, 1), :] * py
        else:
            plane[pl.ds(k * h, h), :] = jnp.zeros((h, count), f32)

    big, small = [], []
    for c in range(3):
        for t in range(tiles):
            cols = slice(t * run, (t + 1) * run)
            block = reach_z[:, cols] * mem[c : c + 1, cols]
            rounded = block.astype(bf16).astype(f32)
            for out, value in ((big, rounded), (small, block - rounded)):
                out.append(jnp.concatenate([value if t == s else zeros for s in range(tiles)], axis=1))
    pad = [jnp.zeros((run - 3 * tiles * window, count), f32)]
    spread = transposed_dot(halves(plane[...]), jnp.concatenate(big + pad + small + pad, axis=0).astype(bf16))
    spread = spread[0:rows] + spread[rows : 2 * rows]
    comb[...] = spread[:, 0:run] + spread[:, run : 2 * run]
    for n in range(6):
        move(comb, [plan.row(x, y) for x, y in plan.force[n]], fs[n], list(range(plan.force_rows[n])))
    for i, g in enumerate(groups):

        @pl.when(lead[i] == 0)
        def _():
            for n in g:
                force_copies[n].start()

    for i in (2, 3, 0, 1):

        @pl.when(lead[i] == 1)
        def _():
            for n in groups[i]:
                pl.semaphore_wait(ready.at[n], 1)
                macro_copies[n].start()
                force_copies[n].start()

    gap = wrap(lax.broadcasted_iota(jnp.int32, (depth, count), 0) - (base[2:3, :] - 1), depth)
    z_high, z_low = split(pick4(gap, [w[2:3] for w in weights]))
    along[pl.ds(0, depth), :] = z_high
    along[pl.ds(depth, depth), :] = z_low

    comp_of = lane // (window * tiles)

    def mark(ones, s, zrow):
        at = jnp.where(lax.broadcasted_iota(jnp.int32, (depth, run), 0).astype(f32) == zrow, 1.0, 0.0)
        for c in range(3):
            ones[pl.ds(c * depth, depth), pl.ds(s * run, run)] = jnp.where(comp_of == c, at, 0.0).astype(bf16)

    def take_macro(n):
        macro_copies[n].wait_recv()
        cells, close, d = plan.edge[n], plan.near[n], sides[n]
        for k in range(4):
            move(
                mr[n],
                [k * len(cells) + i for i in range(len(cells))],
                mac,
                [k * rows + plan.there(c, d) for c in cells],
            )
        return mr[n][pl.ds(plan.macro_rows[n] - 1, 1), :]

    def pop_row(n, q, cell):
        cells, close = plan.edge[n], plan.near[n]
        return 4 * len(cells) + plan.dirs[n].index(q) * len(close) + close.index(cell)

    keep = 1.0 - 1.0 / relax_time
    half = 1.0 - 0.5 / relax_time
    level_row = lax.broadcasted_iota(jnp.int32, (h, 1), 0)

    def population(q, x):
        c = lattice_speeds[q]
        if x < 0 or x >= wx:
            return edge_pops[pl.ds(q * h, h), :]
        value = pops[pl.ds(q * own + x * wy, h), :]
        if c[1] == 1:
            value = jnp.where(level_row == h - 1, mr[4][pl.ds(pop_row(4, q, (x, wy - 1)), 1), :], value)
        if c[1] == -1:
            value = jnp.where(level_row == wy, mr[5][pl.ds(pop_row(5, q, (x, 0)), 1), :], value)
        return value

    def collide(x):
        at = (x + 1) * h
        density = mac[pl.ds(at, h), :]
        force = [grid[pl.ds(k * rows + at, h), :] for k in range(3)]
        inverse = 1.0 / density
        speed = [(mac[pl.ds((k + 1) * rows + at, h), :] + 0.5 * force[k]) * inverse for k in range(3)]
        for k in range(3):
            vel[pl.ds(k * rows + at, h), :] = jnp.where((level_row <= wy + 1) | (level_row == h - 1), speed[k], 0.0)
        square = speed[0] * speed[0] + speed[1] * speed[1] + speed[2] * speed[2]
        work = speed[0] * force[0] + speed[1] * force[1] + speed[2] * force[2]
        scaled = density * (1.0 / relax_time)
        level = scaled * (1.0 - 1.5 * square) - (3.0 * half) * work
        for first in [0] + list(range(1, 19, 2)):
            pair = [0] if first == 0 else [first, first + 1]
            pair = [q for q in pair if 0 <= x + lattice_speeds[q][0] < wx]
            if not pair:
                continue
            weight = lattice_weights[first]
            if first == 0:
                even, odd = level * weight, None
            else:
                a = along_speed(lattice_speeds[first], speed)
                push = along_speed(lattice_speeds[first], force)
                turn = scaled * a + half * push
                even = weight * (level + a * (4.5 * scaled * a + 9.0 * half * push))
                odd = (3.0 * weight) * turn
            for q in pair:
                c = lattice_speeds[q]
                value = keep * population(q, x) + even
                if odd is not None:
                    value = value + odd if q == first else value - odd
                if c[1]:
                    value = pltpu.roll(value, c[1] % h, 0)
                if c[2]:
                    value = pltpu.roll(value, c[2] % depth, 1)
                fresh[pl.ds(q * own + (x + c[0]) * wy, wy), :] = value[0:wy]

    mark(ones_y, 0, zmap)
    for s, n in ((1, 4), (2, 5)):
        mark(ones_y, s, take_macro(n))
    for n in (4, 5):
        force_copies[n].wait_recv()
        move(fr[n], list(range(plan.force_rows[n])), placed[n], [plan.there(c, sides[n]) for c in plan.force[n]])

    def widen(parts, ones):
        value = transposed_dot(halves(jnp.concatenate(parts, axis=1)), ones[...])
        half_rows = value.shape[0] // 2
        return value[0:half_rows] + value[half_rows:]

    value = widen([comb[...], placed[4][...], placed[5][...]], ones_y)
    for c in range(3):
        grid[pl.ds(c * rows, rows), :] = value[:, c * depth : (c + 1) * depth]
    for x in plan.xs:
        if not plan.late(x):
            collide(x)

    edge_rows = {-1: 6, 1: 7}
    for ones, order in ((ones_l, (6, 0, 1)), (ones_r, (7, 2, 3))):
        for s, n in enumerate(order):
            mark(ones, s, take_macro(n))
            for q in plan.dirs[n]:
                for s_cell in plan.near[n]:
                    pass
                close = plan.near[n]
                src = [pop_row(n, q, c) for c in close]
                dst = [q * h + (c[1] - sides[n][1] * wy) % h for c in close]
                move(mr[n], src, edge_pops, dst)
    for ones, order in ((ones_l, (6, 0, 1)), (ones_r, (7, 2, 3))):
        for n in order:
            force_copies[n].wait_recv()
            if n < 4:
                at = 0 if sides[n][0] == 1 else wx * h
                dst = [plan.there(c, sides[n]) - at for c in plan.force[n]]
                move(fr[n], list(range(plan.force_rows[n])), placed[n], dst)
        value = widen([fr[order[0]][...], placed[order[1]][...], placed[order[2]][...]], ones)
        at = 0 if ones is ones_l else wx * h
        for c in range(3):
            here = pl.ds(c * rows + at, 3 * h)
            grid[here, :] = grid[here, :] + value[:, c * depth : (c + 1) * depth]
    for x in plan.xs:
        if plan.late(x):
            collide(x)
    spare = rows - plan.cols * h
    if spare:
        for k in range(3):
            vel[pl.ds(k * rows + plan.cols * h, spare), :] = jnp.zeros((spare, depth), f32)

    for copy in macro_copies + force_copies:
        copy.wait_send()


def finish_kernel(plan, fresh, vel, plane, along, fresh_out, sampled_out, sampled, sems):
    rows, own = plan.rows, plan.own
    depth = fresh.shape[1]
    pieces = [list(range(19))[i::4] for i in range(4)]
    cuts = [0, 5, 10, 15, 19]
    leave = [
        pltpu.make_async_copy(
            fresh.at[pl.ds(a * own, (b - a) * own), :], fresh_out.at[pl.ds(a * own, (b - a) * own), :], sems.at[i]
        )
        for i, (a, b) in enumerate(zip(cuts, cuts[1:]))
    ]
    for copy in leave:
        copy.start()
    last = pltpu.make_async_copy(sampled, sampled_out, sems.at[4])
    v_high, v_low = split(vel[...])
    value = jnp.dot(v_high, along[pl.ds(0, depth), :], preferred_element_type=f32)
    value = value + jnp.dot(v_low, along[pl.ds(0, depth), :], preferred_element_type=f32)
    value = value + jnp.dot(v_high, along[pl.ds(depth, depth), :], preferred_element_type=f32)
    flat = plane[...]
    for k in range(3):
        sampled[k : k + 1, :] = jnp.sum(value[k * rows : (k + 1) * rows] * flat, axis=0, keepdims=True)
    last.start()
    for copy in leave + [last]:
        copy.wait()


def solution(mesh):
    nx, ny = mesh.shape["gx"], mesh.shape["gy"]

    def per_device(populations, vert_base, vert_frac, edges, stiffness, rest):
        _, wx, wy, depth = populations.shape
        count, edge_count = vert_base.shape[1], edges.shape[1]
        plan = Plan(wx, wy)
        rows, tiles, h = plan.rows, count // run, plan.h
        macro = [pltpu.VMEM((n, depth), f32) for n in plan.macro_rows]
        force = [pltpu.VMEM((n, run), f32) for n in plan.force_rows]
        scratch = macro + macro + force + force
        scratch += [
            pltpu.VMEM((19 * wx * wy + h, depth), f32),
            pltpu.VMEM((3, count), jnp.int32),
            pltpu.VMEM((3, count), f32),
            pltpu.VMEM((2, edge_count), jnp.int32),
            pltpu.VMEM((edge_count,), f32),
            pltpu.VMEM((3, edge_count), f32),
            pltpu.VMEM((24 * tiles, run), f32),
            pltpu.VMEM((8, edge_count), f32),
            pltpu.VMEM((8, count), f32),
            pltpu.VMEM((4 * rows, depth), f32),
            pltpu.VMEM((3 * rows, depth), f32),
            pltpu.VMEM((rows, run), f32),
            pltpu.VMEM((up(plan.cols, 8), count), f32),
        ]
        scratch += [pltpu.VMEM((rows if n in (4, 5) else 3 * h, run), f32) for n in range(8)]
        scratch += [pltpu.VMEM((3 * depth, 3 * run), bf16) for _ in range(3)]
        scratch += [
            pltpu.VMEM((19 * h, depth), f32),
            pltpu.SemaphoreType.DMA((4, 8)),
            pltpu.SemaphoreType.DMA((6,)),
            pltpu.SemaphoreType.REGULAR((8,)),
        ]
        vmem = pl.BlockSpec(memory_space=pltpu.VMEM)
        far = pl.BlockSpec(memory_space=pltpu.HBM)

        def exchange(*refs):
            exchange_kernel(plan, nx, ny, *refs)

        def finish(*refs):
            finish_kernel(plan, *refs)

        held = pl.pallas_call(
            exchange,
            out_shape=(
                jax.ShapeDtypeStruct((19 * wx * wy, depth), f32),
                jax.ShapeDtypeStruct((3 * rows, depth), f32),
                jax.ShapeDtypeStruct((rows, count), f32),
                jax.ShapeDtypeStruct((2 * depth, count), bf16),
            ),
            in_specs=[far] * 6,
            out_specs=(vmem,) * 4,
            scratch_shapes=scratch,
            compiler_params=pltpu.CompilerParams(
                collective_id=0, has_side_effects=True, vmem_limit_bytes=24 * 1024 * 1024
            ),
            name="exchange",
        )(
            *[
                pltpu.with_memory_space_constraint(value, pltpu.HBM)
                for value in (
                    populations.reshape(19 * wx * wy, depth),
                    vert_base,
                    vert_frac,
                    edges,
                    stiffness,
                    rest,
                )
            ]
        )
        fresh, sampled = pl.pallas_call(
            finish,
            out_shape=(
                jax.ShapeDtypeStruct((19 * wx * wy, depth), f32),
                jax.ShapeDtypeStruct((3, count), f32),
            ),
            in_specs=[vmem] * 4,
            out_specs=(far, far),
            scratch_shapes=[pltpu.VMEM((3, count), f32), pltpu.SemaphoreType.DMA((5,))],
            compiler_params=pltpu.CompilerParams(vmem_limit_bytes=24 * 1024 * 1024),
            name="finish",
        )(*held)
        return fresh.reshape(19, wx, wy, depth), sampled

    placed = (
        P(None, "gx", "gy", None),
        P(None, ("gx", "gy")),
        P(None, ("gx", "gy")),
        P(None, ("gx", "gy")),
        P(("gx", "gy")),
        P(None, ("gx", "gy")),
    )
    return jax.shard_map(
        per_device,
        mesh=mesh,
        in_specs=placed,
        out_specs=(P(None, "gx", "gy", None), P(None, ("gx", "gy"))),
        check_vma=False,
    )
```

time: 14.9 us -> 13.3 us (0.89)
  Pallas kernels: 14 us -> 12.4 us
    pallas_call x1, Pallas kernels: 12.6 us -> 11.2 us  [per_device(): pl.pallas_call(exchange, out_shape=(jax.ShapeDtypeStruct((19 * wx * wy, d...]
    pallas_call x1, Pallas kernels: 1.43 us -> 1.18 us  [per_device(): pl.pallas_call(finish, out_shape=(jax.ShapeDtypeStruct((19 * wx * wy, dep...]
where the time goes in v1:
time: 13.3 us; the launch traced here: 13.1 us
  Pallas kernels  12.4 us (93%)
  between operations  0.64 us (5%)
    pallas_call x1, Pallas kernels, per_device(): pl.pallas_call(exchange, out_shape=(jax.ShapeDtypeStruct((19 * wx * wy, d...  11.2 us
    pallas_call x1, Pallas kernels, per_device(): pl.pallas_call(finish, out_shape=(jax.ShapeDtypeStruct((19 * wx * wy, dep...  1.18 us

profile of v1, /device:TPU:0, one launch (start us, length us, event | category | flops | bytes accessed | tf_op | source)
XLA Modules:
  0.0 13.1 jit_solution(2007104543313109386)
XLA Ops:
  0.6 11.2 %exchange.1 = (f32[1216,128]{1,0:T(8,128)S(1)}, f32[480,128]{1,0:T(8,128)S(1)}, f32[160,512]{1,0:T(8,128)S(1)}, bf16[256,512]{1,0:T(8,128)(2,1)S(1)}) custom-call(f32[1216,128]{1,0:T(8,128)} %bitcast.2, s32[3,512]{1,0:T(4,128)} %refs_1_.1, f32[3,512]{1,0:T(4,128)} %refs_2_.1, s32[2,1536]{1,0:T(2,128)} %refs_3_.1, f32[1536]{0:T(1024)} %refs_4_.1, ...), custom_call_target="tpu_custom_call" | custom-call | tf_op jit(solution)/shard_map/exchange/pallas_call | solution.py:559
  11.9 1.2 %finish.1 = (f32[1216,128]{1,0:T(8,128)}, f32[3,512]{1,0:T(4,128)}) custom-call(f32[1216,128]{1,0:T(8,128)S(1)} %get-tuple-element.8.refs_0_, f32[480,128]{1,0:T(8,128)S(1)} %get-tuple-element.9.refs_1_, f32[160,512]{1,0:T(8,128)S(1)} %get-tuple-element.10.refs_2_, bf16[256,512]{1,0:T(8,128)(2,1)S(1)} %get-tuple-element.11.refs_3_), custom_call_target="tpu_custom_call" | custom-call | tf_op jit(solution)/shard_map/finish/pallas_call | solution.py:587

commit v2 on v1

--- a/solution.py
+++ b/solution.py
@@ -155,12 +155,11 @@
 
 def exchange_kernel(plan, nx, ny, *refs):
     wx, wy, h, rows, own = plan.wx, plan.wy, plan.h, plan.rows, plan.own
-    sources, results, scratch = refs[0:6], refs[6:10], refs[10:]
-    fresh, vel, plane, along = results
+    sources, (fresh, sampled), scratch = refs[0:6], refs[6:8], refs[8:]
     ms, mr, fs, fr = scratch[0:8], scratch[8:16], scratch[16:24], scratch[24:32]
     (pops, base, frac, edges, stiff, rest, pos, pull, mem, mac, grid, comb, px_ref) = scratch[32:45]
     placed = scratch[45:53]
-    ones_y, ones_l, ones_r, edge_pops, sems, load_sems, ready = scratch[53:]
+    ones_y, ones_l, ones_r, edge_pops, vel, plane, along, part_sum, sems, load_sems, ready = scratch[53:]
     depth = pops.shape[1]
     load_into = (pops.at[pl.ds(0, 19 * own), :], base, frac, edges, stiff, rest)
     loads_in = [pltpu.make_async_copy(sources[n], load_into[n], load_sems.at[n]) for n in range(6)]
@@ -171,40 +170,31 @@
     tiles = count // run
     ix, iy = lax.axis_index("gx"), lax.axis_index("gy")
     peers = [(lax.rem(ix + dx + nx, nx), lax.rem(iy + dy + ny, ny)) for dx, dy in sides]
-    key = ix * ny + iy
-    lead = [(key < peers[g[0]][0] * ny + peers[g[0]][1]).astype(jnp.int32) for g in groups]
+
+    def rank(px, py):
+        return px * ny + py
+
+    key = rank(ix, iy)
+    lead = [(key < rank(px, py)).astype(jnp.int32) for px, py in peers]
+    led = [sum(lead[n] for n in g) for g in groups]
     barrier = pltpu.get_barrier_semaphore()
 
     def hail(sem, n):
         pl.semaphore_signal(sem, inc=1, device_id=peers[n], device_id_type=pl.DeviceIdType.MESH)
 
-    for i, g in enumerate(groups):
-
-        @pl.when(lead[i] == 1)
+    for n in range(8):
+
+        @pl.when(lead[n] == 1)
         def _():
-            for n in g:
-                hail(barrier, n)
-
-    greetings = sum((1 - lead[i]) * len(g) for i, g in enumerate(groups))
-
-    @pl.when(greetings > 0)
-    def _():
-        pl.semaphore_wait(barrier, greetings)
-
-    for i, g in enumerate(groups):
-
-        @pl.when(lead[i] == 0)
-        def _():
-            for n in g:
-                hail(ready.at[sides.index((-sides[n][0], -sides[n][1]))], n)
+            hail(barrier, n)
 
     def copies(src, dst, kind):
         return [
             pltpu.make_async_remote_copy(
                 src_ref=src[n],
                 dst_ref=dst[n],
-                send_sem=sems.at[kind, n],
-                recv_sem=sems.at[kind + 1, n],
+                send_sem=sems.at[0],
+                recv_sem=sems.at[kind + (0 if n in (4, 5) else 1)],
                 device_id=peers[n],
                 device_id_type=pl.DeviceIdType.MESH,
             )
@@ -215,8 +205,20 @@
     outgoing = list(fs)
     for n in (6, 7):
         outgoing[n] = comb.at[pl.ds(first_col[sides[n][0]] * h, 3 * h), :]
-    macro_copies = copies(ms, mr, 0)
-    force_copies = copies(outgoing, fr, 2)
+    macro_copies = copies(ms, mr, 1)
+    force_copies = copies(outgoing, fr, 3)
+
+    def arrive(kind, which):
+        lengths = plan.macro_rows if kind == 1 else plan.force_rows
+        all_of = pops.at[pl.ds(0, sum(lengths[n] for n in which)), :]
+        pltpu.make_async_remote_copy(
+            src_ref=all_of,
+            dst_ref=all_of,
+            send_sem=sems.at[0],
+            recv_sem=sems.at[kind + (0 if 4 in which else 1)],
+            device_id=peers[0],
+            device_id_type=pl.DeviceIdType.MESH,
+        ).wait_recv()
 
     zeros = jnp.zeros((8, run), f32)
     pos[...] = jnp.zeros(pos.shape, f32)
@@ -250,38 +252,6 @@
     offset = jnp.concatenate(offsets, axis=1)
     reach_z = pick4(lax.broadcasted_iota(jnp.int32, (window, count), 0) - offset, [w[2:3] for w in weights])
 
-    loads_in[0].wait()
-    for r in range(0, own, 8):
-        totals = [None] * 4
-        for q, c in enumerate(lattice_speeds):
-            value = pops[pl.ds(q * own + r, 8), :]
-            for k, sign in enumerate((1,) + c):
-                if sign:
-                    term = value if sign > 0 else -value
-                    totals[k] = term if totals[k] is None else totals[k] + term
-        for k in range(4):
-            for i in range(0, 8, wy):
-                mac[pl.ds(k * rows + plan.row((r + i) // wy, 0), wy), :] = totals[k][i : i + wy]
-    for n in range(8):
-        cells, close = plan.edge[n], plan.near[n]
-        for k in range(4):
-            move(
-                mac,
-                [k * rows + plan.row(x, y) for x, y in cells],
-                ms[n],
-                [k * len(cells) + i for i in range(len(cells))],
-            )
-        for s, q in enumerate(plan.dirs[n]):
-            first = 4 * len(cells) + s * len(close)
-            move(pops, [q * own + x * wy + y for x, y in close], ms[n], [first + i for i in range(len(close))])
-        ms[n][pl.ds(plan.macro_rows[n] - 1, 1), :] = zmap
-    for i, g in enumerate(groups):
-
-        @pl.when(lead[i] == 0)
-        def _():
-            for n in g:
-                macro_copies[n].start()
-
     part = 8 * tiles
     high = moved.astype(bf16).astype(f32)
     low = moved - high
@@ -299,6 +269,39 @@
     group = lax.shift_right_logical(ends[0:1], run.bit_length() - 1)
     reach = jnp.dot(pos[...].astype(bf16), hot, preferred_element_type=f32)
     reach = reach[0:part] + reach[part : 2 * part] + reach[2 * part : 3 * part]
+    def moments(r):
+        totals = [None] * 4
+        for q, c in enumerate(lattice_speeds):
+            value = pops[pl.ds(q * own + r, 8), :]
+            for k, sign in enumerate((1,) + c):
+                if sign:
+                    term = value if sign > 0 else -value
+                    totals[k] = term if totals[k] is None else totals[k] + term
+        for k in range(4):
+            for i in range(0, 8, wy):
+                mac[pl.ds(k * rows + plan.row((r + i) // wy, 0), wy), :] = totals[k][i : i + wy]
+
+    def pack(n):
+        cells, close = plan.edge[n], plan.near[n]
+        for k in range(4):
+            move(
+                mac,
+                [k * rows + plan.row(x, y) for x, y in cells],
+                ms[n],
+                [k * len(cells) + i for i in range(len(cells))],
+            )
+        for s, q in enumerate(plan.dirs[n]):
+            first = 4 * len(cells) + s * len(close)
+            move(pops, [q * own + x * wy + y for x, y in close], ms[n], [first + i for i in range(len(close))])
+        ms[n][pl.ds(plan.macro_rows[n] - 1, 1), :] = zmap
+
+    late = (0, 1, 6, 2, 3, 7)
+    ends_of = sorted({x * wy // 8 * 8 for x in (0, 1, wx - 1)})
+    loads_in[0].wait()
+    for r in ends_of:
+        moments(r)
+    for n in late:
+        pack(n)
     pull[pl.ds(0, 3), :] = rest[...]
     diff = jnp.zeros((8, edge_count), f32)
     for t in range(tiles):
@@ -337,21 +340,57 @@
     comb[...] = spread[:, 0:run] + spread[:, run : 2 * run]
     for n in range(6):
         move(comb, [plan.row(x, y) for x, y in plan.force[n]], fs[n], list(range(plan.force_rows[n])))
-    for i, g in enumerate(groups):
-
-        @pl.when(lead[i] == 0)
+    greetings = 8 - sum(lead)
+
+    @pl.when(greetings > 0)
+    def _():
+        pl.semaphore_wait(barrier, greetings)
+
+    for n in range(8):
+        back = sides.index((-sides[n][0], -sides[n][1]))
+        slot_of = [i for i, g in enumerate(groups) if back in g][0]
+
+        @pl.when(lead[n] == 0)
         def _():
-            for n in g:
+            hail(ready.at[slot_of], n)
+
+    for n in late:
+
+        @pl.when(lead[n] == 0)
+        def _():
+            force_copies[n].start()
+            macro_copies[n].start()
+
+    for n in (4, 5):
+
+        @pl.when(lead[n] == 0)
+        def _():
+            force_copies[n].start()
+
+    for r in range(0, own, 8):
+        if r not in ends_of:
+            moments(r)
+    for n in (4, 5):
+        pack(n)
+
+    for n in (4, 5):
+
+        @pl.when(lead[n] == 0)
+        def _():
+            macro_copies[n].start()
+
+    for i in (2, 3, 0, 1):
+
+        @pl.when(led[i] > 0)
+        def _():
+            pl.semaphore_wait(ready.at[i], led[i])
+
+        for n in groups[i]:
+
+            @pl.when(lead[n] == 1)
+            def _():
                 force_copies[n].start()
-
-    for i in (2, 3, 0, 1):
-
-        @pl.when(lead[i] == 1)
-        def _():
-            for n in groups[i]:
-                pl.semaphore_wait(ready.at[n], 1)
                 macro_copies[n].start()
-                force_copies[n].start()
 
     gap = wrap(lax.broadcasted_iota(jnp.int32, (depth, count), 0) - (base[2:3, :] - 1), depth)
     z_high, z_low = split(pick4(gap, [w[2:3] for w in weights]))
@@ -359,14 +398,17 @@
     along[pl.ds(depth, depth), :] = z_low
 
     comp_of = lane // (window * tiles)
+    comps_of = jnp.concatenate([comp_of] * 3, axis=1)
 
     def mark(ones, s, zrow):
         at = jnp.where(lax.broadcasted_iota(jnp.int32, (depth, run), 0).astype(f32) == zrow, 1.0, 0.0)
+        if ones.shape[0] == depth:
+            ones[:, pl.ds(s * run, run)] = at.astype(bf16)
+            return
         for c in range(3):
             ones[pl.ds(c * depth, depth), pl.ds(s * run, run)] = jnp.where(comp_of == c, at, 0.0).astype(bf16)
 
     def take_macro(n):
-        macro_copies[n].wait_recv()
         cells, close, d = plan.edge[n], plan.near[n], sides[n]
         for k in range(4):
             move(
@@ -403,7 +445,8 @@
         inverse = 1.0 / density
         speed = [(mac[pl.ds((k + 1) * rows + at, h), :] + 0.5 * force[k]) * inverse for k in range(3)]
         for k in range(3):
-            vel[pl.ds(k * rows + at, h), :] = jnp.where((level_row <= wy + 1) | (level_row == h - 1), speed[k], 0.0)
+            held = jnp.where((level_row <= wy + 1) | (level_row == h - 1), speed[k], 0.0)
+            vel[pl.ds(k * rows + at, h), :] = held
         square = speed[0] * speed[0] + speed[1] * speed[1] + speed[2] * speed[2]
         work = speed[0] * force[0] + speed[1] * force[1] + speed[2] * force[2]
         scaled = density * (1.0 / relax_time)
@@ -434,10 +477,11 @@
                 fresh[pl.ds(q * own + (x + c[0]) * wy, wy), :] = value[0:wy]
 
     mark(ones_y, 0, zmap)
+    arrive(1, (4, 5))
     for s, n in ((1, 4), (2, 5)):
         mark(ones_y, s, take_macro(n))
+    arrive(3, (4, 5))
     for n in (4, 5):
-        force_copies[n].wait_recv()
         move(fr[n], list(range(plan.force_rows[n])), placed[n], [plan.there(c, sides[n]) for c in plan.force[n]])
 
     def widen(parts, ones):
@@ -452,64 +496,78 @@
         if not plan.late(x):
             collide(x)
 
-    edge_rows = {-1: 6, 1: 7}
+    def sample(spans):
+        flat = jnp.concatenate([plane[pl.ds(a, n), :] for a, n in spans], axis=0)
+        value = jnp.concatenate([vel[pl.ds(k * rows + a, n), :] for k in range(3) for a, n in spans], axis=0)
+        v_high, v_low = split(value)
+        value = jnp.dot(
+            jnp.concatenate(
+                [
+                    jnp.concatenate([v_high, v_high], axis=1),
+                    jnp.concatenate([v_low, jnp.zeros(v_low.shape, bf16)], axis=1),
+                ],
+                axis=0,
+            ),
+            along[...],
+            preferred_element_type=f32,
+        )
+        size = flat.shape[0]
+        out = []
+        for k in range(3):
+            both = value[k * size : (k + 1) * size] + value[(k + 3) * size : (k + 4) * size]
+            both = both * flat
+            acc = both[0:8]
+            for r in range(8, size, 8):
+                acc = acc + both[r : r + 8]
+            out.append(acc)
+        return out
+
+    left, right = 3 * h, wx * h
+    for k, value in enumerate(sample([(left, right - left)])):
+        part_sum[pl.ds(8 * k, 8), :] = value
+
+    arrive(1, late)
     for ones, order in ((ones_l, (6, 0, 1)), (ones_r, (7, 2, 3))):
         for s, n in enumerate(order):
             mark(ones, s, take_macro(n))
             for q in plan.dirs[n]:
-                for s_cell in plan.near[n]:
-                    pass
                 close = plan.near[n]
                 src = [pop_row(n, q, c) for c in close]
-                dst = [q * h + (c[1] - sides[n][1] * wy) % h for c in close]
-                move(mr[n], src, edge_pops, dst)
-    for ones, order in ((ones_l, (6, 0, 1)), (ones_r, (7, 2, 3))):
-        for n in order:
-            force_copies[n].wait_recv()
-            if n < 4:
-                at = 0 if sides[n][0] == 1 else wx * h
-                dst = [plan.there(c, sides[n]) - at for c in plan.force[n]]
-                move(fr[n], list(range(plan.force_rows[n])), placed[n], dst)
-        value = widen([fr[order[0]][...], placed[order[1]][...], placed[order[2]][...]], ones)
-        at = 0 if ones is ones_l else wx * h
+                move(mr[n], src, edge_pops, [q * h + (c[1] - sides[n][1] * wy) % h for c in close])
+    arrive(3, late)
+    for ones, order, at in ((ones_l, (6, 0, 1), 0), (ones_r, (7, 2, 3), right)):
+        for n in order[1:]:
+            dst = [plan.there(c, sides[n]) - at for c in plan.force[n]]
+            move(fr[n], list(range(plan.force_rows[n])), placed[n], dst)
+        parts = jnp.concatenate([fr[order[0]][...], placed[order[1]][...], placed[order[2]][...]], axis=1)
+        parts = jnp.concatenate([jnp.where(comps_of == c, parts, 0.0) for c in range(3)], axis=0)
+        value = transposed_dot(halves(parts), ones[...])
         for c in range(3):
             here = pl.ds(c * rows + at, 3 * h)
-            grid[here, :] = grid[here, :] + value[:, c * depth : (c + 1) * depth]
+            both = value[3 * h * c : 3 * h * (c + 1)] + value[3 * h * (c + 3) : 3 * h * (c + 4)]
+            grid[here, :] = grid[here, :] + both
     for x in plan.xs:
         if plan.late(x):
             collide(x)
-    spare = rows - plan.cols * h
-    if spare:
-        for k in range(3):
-            vel[pl.ds(k * rows + plan.cols * h, spare), :] = jnp.zeros((spare, depth), f32)
-
-    for copy in macro_copies + force_copies:
-        copy.wait_send()
-
-
-def finish_kernel(plan, fresh, vel, plane, along, fresh_out, sampled_out, sampled, sems):
-    rows, own = plan.rows, plan.own
-    depth = fresh.shape[1]
-    pieces = [list(range(19))[i::4] for i in range(4)]
-    cuts = [0, 5, 10, 15, 19]
-    leave = [
-        pltpu.make_async_copy(
-            fresh.at[pl.ds(a * own, (b - a) * own), :], fresh_out.at[pl.ds(a * own, (b - a) * own), :], sems.at[i]
-        )
-        for i, (a, b) in enumerate(zip(cuts, cuts[1:]))
-    ]
+    for k, value in enumerate(sample([(0, left), (right, 3 * h)])):
+        value = value + part_sum[pl.ds(8 * k, 8), :]
+        sampled[k : k + 1, :] = jnp.sum(value, axis=0, keepdims=True)
+    sent = pops.at[pl.ds(0, sum(plan.macro_rows) + sum(plan.force_rows)), :]
+    pltpu.make_async_remote_copy(
+        src_ref=sent,
+        dst_ref=sent,
+        send_sem=sems.at[0],
+        recv_sem=sems.at[1],
+        device_id=peers[0],
+        device_id_type=pl.DeviceIdType.MESH,
+    ).wait_send()
+
+
+def finish_kernel(fresh, sampled, fresh_out, sampled_out, sems):
+    leave = [pltpu.make_async_copy(fresh, fresh_out, sems.at[0]), pltpu.make_async_copy(sampled, sampled_out, sems.at[1])]
     for copy in leave:
         copy.start()
-    last = pltpu.make_async_copy(sampled, sampled_out, sems.at[4])
-    v_high, v_low = split(vel[...])
-    value = jnp.dot(v_high, along[pl.ds(0, depth), :], preferred_element_type=f32)
-    value = value + jnp.dot(v_low, along[pl.ds(0, depth), :], preferred_element_type=f32)
-    value = value + jnp.dot(v_high, along[pl.ds(depth, depth), :], preferred_element_type=f32)
-    flat = plane[...]
-    for k in range(3):
-        sampled[k : k + 1, :] = jnp.sum(value[k * rows : (k + 1) * rows] * flat, axis=0, keepdims=True)
-    last.start()
-    for copy in leave + [last]:
+    for copy in leave:
         copy.wait()
 
 
@@ -540,32 +598,31 @@
             pltpu.VMEM((up(plan.cols, 8), count), f32),
         ]
         scratch += [pltpu.VMEM((rows if n in (4, 5) else 3 * h, run), f32) for n in range(8)]
-        scratch += [pltpu.VMEM((3 * depth, 3 * run), bf16) for _ in range(3)]
+        scratch += [pltpu.VMEM((n * depth, 3 * run), bf16) for n in (3, 1, 1)]
         scratch += [
             pltpu.VMEM((19 * h, depth), f32),
-            pltpu.SemaphoreType.DMA((4, 8)),
+            pltpu.VMEM((3 * rows, depth), f32),
+            pltpu.VMEM((rows, count), f32),
+            pltpu.VMEM((2 * depth, count), bf16),
+            pltpu.VMEM((24, count), f32),
+            pltpu.SemaphoreType.DMA((5,)),
             pltpu.SemaphoreType.DMA((6,)),
-            pltpu.SemaphoreType.REGULAR((8,)),
+            pltpu.SemaphoreType.REGULAR((len(groups),)),
         ]
         vmem = pl.BlockSpec(memory_space=pltpu.VMEM)
         far = pl.BlockSpec(memory_space=pltpu.HBM)
 
         def exchange(*refs):
             exchange_kernel(plan, nx, ny, *refs)
-
-        def finish(*refs):
-            finish_kernel(plan, *refs)
 
         held = pl.pallas_call(
             exchange,
             out_shape=(
                 jax.ShapeDtypeStruct((19 * wx * wy, depth), f32),
-                jax.ShapeDtypeStruct((3 * rows, depth), f32),
-                jax.ShapeDtypeStruct((rows, count), f32),
-                jax.ShapeDtypeStruct((2 * depth, count), bf16),
+                jax.ShapeDtypeStruct((3, count), f32),
             ),
             in_specs=[far] * 6,
-            out_specs=(vmem,) * 4,
+            out_specs=(vmem,) * 2,
             scratch_shapes=scratch,
             compiler_params=pltpu.CompilerParams(
                 collective_id=0, has_side_effects=True, vmem_limit_bytes=24 * 1024 * 1024
@@ -585,14 +642,14 @@
             ]
         )
         fresh, sampled = pl.pallas_call(
-            finish,
+            finish_kernel,
             out_shape=(
                 jax.ShapeDtypeStruct((19 * wx * wy, depth), f32),
                 jax.ShapeDtypeStruct((3, count), f32),
             ),
-            in_specs=[vmem] * 4,
+            in_specs=[vmem] * 2,
             out_specs=(far, far),
-            scratch_shapes=[pltpu.VMEM((3, count), f32), pltpu.SemaphoreType.DMA((5,))],
+            scratch_shapes=[pltpu.SemaphoreType.DMA((2,))],
             compiler_params=pltpu.CompilerParams(vmem_limit_bytes=24 * 1024 * 1024),
             name="finish",
         )(*held)

time: 13.3 us -> 12.2 us (0.917)
  Pallas kernels: 12.4 us -> 11.3 us
    pallas_call x1, Pallas kernels: 11.2 us -> 10.5 us  [per_device(): pl.pallas_call(exchange, out_shape=(jax.ShapeDtypeStruct((19 * wx * wy, d...]
    pallas_call x1, Pallas kernels: 1.18 us -> 0.85 us  [per_device(): pl.pallas_call(finish_kernel, out_shape=(jax.ShapeDtypeStruct((19 * wx *...]
where the time goes in v2:
time: 12.2 us; the launch traced here: 11.9 us
  Pallas kernels  11.3 us (93%)
  between operations  0.64 us (5%)
    pallas_call x1, Pallas kernels, per_device(): pl.pallas_call(exchange, out_shape=(jax.ShapeDtypeStruct((19 * wx * wy, d...  10.5 us
    pallas_call x1, Pallas kernels, per_device(): pl.pallas_call(finish_kernel, out_shape=(jax.ShapeDtypeStruct((19 * wx *...  0.85 us

profile of v2, /device:TPU:0, one launch (start us, length us, event | category | flops | bytes accessed | tf_op | source)
XLA Modules:
  0.0 11.9 jit_solution(15405249785454843603)
XLA Ops:
  0.6 10.5 %exchange.1 = (f32[1216,128]{1,0:T(8,128)S(1)}, f32[3,512]{1,0:T(4,128)S(1)}) custom-call(f32[1216,128]{1,0:T(8,128)} %bitcast.2, s32[3,512]{1,0:T(4,128)} %refs_1_.1, f32[3,512]{1,0:T(4,128)} %refs_2_.1, s32[2,1536]{1,0:T(2,128)} %refs_3_.1, f32[1536]{0:T(1024)} %refs_4_.1, f32[3,1536]{1,0:T(4,128)} %refs_5_.1), custom_call_target="tpu_custom_call" | custom-call | tf_op jit(solution)/shard_map/exchange/pallas_call | solution.py:618
  11.1 0.8 %finish.1 = (f32[1216,128]{1,0:T(8,128)}, f32[3,512]{1,0:T(4,128)}) custom-call(f32[1216,128]{1,0:T(8,128)S(1)} %get-tuple-element.6.fresh, f32[3,512]{1,0:T(4,128)S(1)} %get-tuple-element.7.sampled), custom_call_target="tpu_custom_call" | custom-call | tf_op jit(solution)/shard_map/finish/pallas_call | solution.py:644

commit v3 on v2

--- a/solution.py
+++ b/solution.py
@@ -30,6 +30,7 @@
 relax_time = 0.9
 run = 128
 window = 8
+pieces = 1
 sides = [(1, 1), (1, -1), (-1, 1), (-1, -1), (0, 1), (0, -1), (1, 0), (-1, 0)]
 groups = [(0, 1, 6), (2, 3, 7), (4,), (5,)]
 f32, bf16 = jnp.float32, jnp.bfloat16
@@ -153,13 +154,41 @@
     return lax.dot_general(a, b, (((1,), (1,)), ((), ())), preferred_element_type=f32)
 
 
+def sample(vel, plane, along, rows, spans):
+    flat = jnp.concatenate([plane[pl.ds(a, n), :] for a, n in spans], axis=0)
+    value = jnp.concatenate([vel[pl.ds(k * rows + a, n), :] for k in range(3) for a, n in spans], axis=0)
+    v_high, v_low = split(value)
+    value = jnp.dot(
+        jnp.concatenate(
+            [
+                jnp.concatenate([v_high, v_high], axis=1),
+                jnp.concatenate([v_low, jnp.zeros(v_low.shape, bf16)], axis=1),
+            ],
+            axis=0,
+        ),
+        along[...],
+        preferred_element_type=f32,
+    )
+    size = flat.shape[0]
+    out = []
+    for k in range(3):
+        both = value[k * size : (k + 1) * size] + value[(k + 3) * size : (k + 4) * size]
+        both = both * flat
+        acc = both[0:8]
+        for r in range(8, size, 8):
+            acc = acc + both[r : r + 8]
+        out.append(acc)
+    return out
+
+
 def exchange_kernel(plan, nx, ny, *refs):
     wx, wy, h, rows, own = plan.wx, plan.wy, plan.h, plan.rows, plan.own
-    sources, (fresh, sampled), scratch = refs[0:6], refs[6:8], refs[8:]
+    sources, scratch = refs[0:6], refs[11:]
+    fresh, vel, plane, along, part_sum = refs[6:11]
     ms, mr, fs, fr = scratch[0:8], scratch[8:16], scratch[16:24], scratch[24:32]
     (pops, base, frac, edges, stiff, rest, pos, pull, mem, mac, grid, comb, px_ref) = scratch[32:45]
     placed = scratch[45:53]
-    ones_y, ones_l, ones_r, edge_pops, vel, plane, along, part_sum, sems, load_sems, ready = scratch[53:]
+    ones_y, ones_l, ones_r, edge_pops, sems, load_sems, ready = scratch[53:]
     depth = pops.shape[1]
     load_into = (pops.at[pl.ds(0, 19 * own), :], base, frac, edges, stiff, rest)
     loads_in = [pltpu.make_async_copy(sources[n], load_into[n], load_sems.at[n]) for n in range(6)]
@@ -221,6 +250,7 @@
         ).wait_recv()
 
     zeros = jnp.zeros((8, run), f32)
+    comb[...] = jnp.zeros(comb.shape, f32)
     pos[...] = jnp.zeros(pos.shape, f32)
     pull[...] = jnp.zeros(pull.shape, f32)
     for ref in placed:
@@ -252,23 +282,36 @@
     offset = jnp.concatenate(offsets, axis=1)
     reach_z = pick4(lax.broadcasted_iota(jnp.int32, (window, count), 0) - offset, [w[2:3] for w in weights])
 
-    part = 8 * tiles
-    high = moved.astype(bf16).astype(f32)
-    low = moved - high
-    whole = base[...].astype(f32)
-    for t in range(tiles):
-        cols = slice(t * run, (t + 1) * run)
-        pos[pl.ds(8 * t, 3), :] = whole[:, cols]
-        pos[pl.ds(part + 8 * t, 3), :] = high[:, cols]
-        pos[pl.ds(2 * part + 8 * t, 3), :] = low[:, cols]
+    pairs = up(tiles, 2) // 2
     ends = edges[...]
-    spot = lax.broadcasted_iota(jnp.int32, (run, edge_count), 0)
     tail = jnp.bitwise_and(ends[0:1], run - 1)
     head = jnp.bitwise_and(ends[1:2], run - 1)
+    group = lax.shift_right_logical(ends[0:1], run.bit_length() - 1)
+    whole = base[...].astype(f32) + moved
+    for t in range(tiles):
+        pos[pl.ds(4 * t, 3), :] = whole[:, t * run : (t + 1) * run]
+    for k in (0, 4):
+        pull[pl.ds(k, 3), :] = rest[...]
+    half_of = lax.broadcasted_iota(jnp.int32, (8, edge_count), 0) // 4
+    mine = [group == 2 * p + half_of for p in range(pairs)]
+    diff = jnp.zeros((8, edge_count), f32)
+    for p in range(pairs):
+        table = pos[pl.ds(8 * p, 8), :]
+        gathered = []
+        for k in range(0, edge_count, run):
+            at = [jnp.broadcast_to(value[:, k : k + run], (8, run)) for value in (head, tail)]
+            gathered.append(
+                jnp.take_along_axis(table, at[0], axis=1) - jnp.take_along_axis(table, at[1], axis=1)
+            )
+        diff = jnp.where(mine[p], jnp.concatenate(gathered, axis=1), diff)
+    stretch = stiff[...].reshape(1, edge_count) * (diff - pull[...])
+    terms = jnp.concatenate([jnp.where(mine[p], stretch, 0.0) for p in range(pairs)], axis=0)
+    spot = lax.broadcasted_iota(jnp.int32, (run, edge_count), 0)
     hot = jnp.where(spot == head, 1.0, jnp.where(spot == tail, -1.0, 0.0)).astype(bf16)
-    group = lax.shift_right_logical(ends[0:1], run.bit_length() - 1)
-    reach = jnp.dot(pos[...].astype(bf16), hot, preferred_element_type=f32)
-    reach = reach[0:part] + reach[part : 2 * part] + reach[2 * part : 3 * part]
+    part = 8 * pairs
+    summed = transposed_dot(halves(terms), hot)
+    mem[...] = -(summed[0:part] + summed[part : 2 * part])
+
     def moments(r):
         totals = [None] * 4
         for q, c in enumerate(lattice_speeds):
@@ -296,22 +339,6 @@
         ms[n][pl.ds(plan.macro_rows[n] - 1, 1), :] = zmap
 
     late = (0, 1, 6, 2, 3, 7)
-    ends_of = sorted({x * wy // 8 * 8 for x in (0, 1, wx - 1)})
-    loads_in[0].wait()
-    for r in ends_of:
-        moments(r)
-    for n in late:
-        pack(n)
-    pull[pl.ds(0, 3), :] = rest[...]
-    diff = jnp.zeros((8, edge_count), f32)
-    for t in range(tiles):
-        diff = jnp.where(group == t, reach[8 * t : 8 * t + 8], diff)
-    stretch = stiff[...].reshape(1, edge_count) * (diff - pull[...])
-    terms = jnp.concatenate([jnp.where(group == t, stretch, 0.0) for t in range(tiles)], axis=0)
-    summed = transposed_dot(halves(terms), hot)
-    summed = summed[0:part] + summed[part : 2 * part]
-    for t in range(tiles):
-        mem[:, t * run : (t + 1) * run] = -summed[8 * t : 8 * t + 8]
 
     bx = base[0:1, :] - ix * wx - 1
     by = base[1:2, :] - iy * wy - 1
@@ -320,26 +347,42 @@
     i = lax.broadcasted_iota(jnp.int32, (h, 1), 0)
     y = jnp.where(i == h - 1, -1, jnp.where(i > wy + 1, -100, i))
     py = pick4(y - by, [w[1:2] for w in weights])
-    for k in range(rows // h):
-        if k < plan.cols:
-            plane[pl.ds(k * h, h), :] = px_ref[pl.ds(k, 1), :] * py
-        else:
-            plane[pl.ds(k * h, h), :] = jnp.zeros((h, count), f32)
-
     big, small = [], []
     for c in range(3):
         for t in range(tiles):
             cols = slice(t * run, (t + 1) * run)
-            block = reach_z[:, cols] * mem[c : c + 1, cols]
+            block = reach_z[:, cols] * mem[pl.ds(4 * t + c, 1), :]
             rounded = block.astype(bf16).astype(f32)
             for out, value in ((big, rounded), (small, block - rounded)):
                 out.append(jnp.concatenate([value if t == s else zeros for s in range(tiles)], axis=1))
     pad = [jnp.zeros((run - 3 * tiles * window, count), f32)]
-    spread = transposed_dot(halves(plane[...]), jnp.concatenate(big + pad + small + pad, axis=0).astype(bf16))
-    spread = spread[0:rows] + spread[rows : 2 * rows]
-    comb[...] = spread[:, 0:run] + spread[:, run : 2 * run]
-    for n in range(6):
+    source = jnp.concatenate(big + pad + small + pad, axis=0).astype(bf16)
+
+    def spread(spans):
+        for a, n in spans:
+            for k in range(a // h, (a + n) // h):
+                plane[pl.ds(k * h, h), :] = px_ref[pl.ds(k, 1), :] * py
+        flat = jnp.concatenate([plane[pl.ds(a, n), :] for a, n in spans], axis=0)
+        size = flat.shape[0]
+        value = transposed_dot(halves(flat), source)
+        value = value[0:size] + value[size : 2 * size]
+        value = value[:, 0:run] + value[:, run : 2 * run]
+        done = 0
+        for a, n in spans:
+            comb[pl.ds(a, n), :] = value[done : done + n]
+            done += n
+
+    left, right = 3 * h, wx * h
+    spread([(0, left), (right, 3 * h)])
+    for n in range(4):
         move(comb, [plan.row(x, y) for x, y in plan.force[n]], fs[n], list(range(plan.force_rows[n])))
+    loads_in[0].wait()
+    ends_of = sorted({x * wy // 8 * 8 for x in (0, 1, wx - 1)})
+    for r in ends_of:
+        moments(r)
+    for n in late:
+        pack(n)
+
     greetings = 8 - sum(lead)
 
     @pl.when(greetings > 0)
@@ -358,13 +401,7 @@
 
         @pl.when(lead[n] == 0)
         def _():
-            force_copies[n].start()
             macro_copies[n].start()
-
-    for n in (4, 5):
-
-        @pl.when(lead[n] == 0)
-        def _():
             force_copies[n].start()
 
     for r in range(0, own, 8):
@@ -378,6 +415,15 @@
         @pl.when(lead[n] == 0)
         def _():
             macro_copies[n].start()
+
+    spread([(left, right - left)])
+    for n in (4, 5):
+        move(comb, [plan.row(x, y) for x, y in plan.force[n]], fs[n], list(range(plan.force_rows[n])))
+    for n in (4, 5):
+
+        @pl.when(lead[n] == 0)
+        def _():
+            force_copies[n].start()
 
     for i in (2, 3, 0, 1):
 
@@ -451,25 +497,30 @@
         work = speed[0] * force[0] + speed[1] * force[1] + speed[2] * force[2]
         scaled = density * (1.0 / relax_time)
         level = scaled * (1.0 - 1.5 * square) - (3.0 * half) * work
+        carried = [scaled * speed[k] for k in range(3)]
+        pushed = [half * force[k] for k in range(3)]
+        odd_of = [carried[k] + pushed[k] for k in range(3)]
+        even_of = [odd_of[k] + pushed[k] for k in range(3)]
+        levels, odds, evens = {}, {}, {}
+        for weight in sorted({lattice_weights[q] for q in range(19)}):
+            levels[weight] = weight * level
+            odds[weight] = [(3.0 * weight) * odd_of[k] for k in range(3)]
+            evens[weight] = [(4.5 * weight) * even_of[k] for k in range(3)]
         for first in [0] + list(range(1, 19, 2)):
             pair = [0] if first == 0 else [first, first + 1]
             pair = [q for q in pair if 0 <= x + lattice_speeds[q][0] < wx]
             if not pair:
                 continue
             weight = lattice_weights[first]
-            if first == 0:
-                even, odd = level * weight, None
-            else:
-                a = along_speed(lattice_speeds[first], speed)
-                push = along_speed(lattice_speeds[first], force)
-                turn = scaled * a + half * push
-                even = weight * (level + a * (4.5 * scaled * a + 9.0 * half * push))
-                odd = (3.0 * weight) * turn
+            even, odd = levels[weight], None
+            if first:
+                c = lattice_speeds[first]
+                even = even + along_speed(c, speed) * along_speed(c, evens[weight])
+                odd = along_speed(c, odds[weight])
             for q in pair:
                 c = lattice_speeds[q]
-                value = keep * population(q, x) + even
-                if odd is not None:
-                    value = value + odd if q == first else value - odd
+                total = even if odd is None else even + odd if q == first else even - odd
+                value = keep * population(q, x) + total
                 if c[1]:
                     value = pltpu.roll(value, c[1] % h, 0)
                 if c[2]:
@@ -496,34 +547,7 @@
         if not plan.late(x):
             collide(x)
 
-    def sample(spans):
-        flat = jnp.concatenate([plane[pl.ds(a, n), :] for a, n in spans], axis=0)
-        value = jnp.concatenate([vel[pl.ds(k * rows + a, n), :] for k in range(3) for a, n in spans], axis=0)
-        v_high, v_low = split(value)
-        value = jnp.dot(
-            jnp.concatenate(
-                [
-                    jnp.concatenate([v_high, v_high], axis=1),
-                    jnp.concatenate([v_low, jnp.zeros(v_low.shape, bf16)], axis=1),
-                ],
-                axis=0,
-            ),
-            along[...],
-            preferred_element_type=f32,
-        )
-        size = flat.shape[0]
-        out = []
-        for k in range(3):
-            both = value[k * size : (k + 1) * size] + value[(k + 3) * size : (k + 4) * size]
-            both = both * flat
-            acc = both[0:8]
-            for r in range(8, size, 8):
-                acc = acc + both[r : r + 8]
-            out.append(acc)
-        return out
-
-    left, right = 3 * h, wx * h
-    for k, value in enumerate(sample([(left, right - left)])):
+    for k, value in enumerate(sample(vel, plane, along, rows, [(left, right - left)])):
         part_sum[pl.ds(8 * k, 8), :] = value
 
     arrive(1, late)
@@ -549,9 +573,6 @@
     for x in plan.xs:
         if plan.late(x):
             collide(x)
-    for k, value in enumerate(sample([(0, left), (right, 3 * h)])):
-        value = value + part_sum[pl.ds(8 * k, 8), :]
-        sampled[k : k + 1, :] = jnp.sum(value, axis=0, keepdims=True)
     sent = pops.at[pl.ds(0, sum(plan.macro_rows) + sum(plan.force_rows)), :]
     pltpu.make_async_remote_copy(
         src_ref=sent,
@@ -563,10 +584,20 @@
     ).wait_send()
 
 
-def finish_kernel(fresh, sampled, fresh_out, sampled_out, sems):
-    leave = [pltpu.make_async_copy(fresh, fresh_out, sems.at[0]), pltpu.make_async_copy(sampled, sampled_out, sems.at[1])]
+def finish_kernel(plan, fresh, vel, plane, along, part_sum, fresh_out, sampled_out, sampled, sems):
+    h, size = plan.h, fresh.shape[0]
+    step = up(size // pieces, 8)
+    leave = []
+    for i in range(pieces):
+        here = pl.ds(i * step, min(step, size - i * step))
+        leave.append(pltpu.make_async_copy(fresh.at[here, :], fresh_out.at[here, :], sems.at[i]))
     for copy in leave:
         copy.start()
+    leave.append(pltpu.make_async_copy(sampled, sampled_out, sems.at[pieces]))
+    for k, value in enumerate(sample(vel, plane, along, plan.rows, [(0, 3 * h), (plan.wx * h, 3 * h)])):
+        value = value + part_sum[pl.ds(8 * k, 8), :]
+        sampled[k : k + 1, :] = jnp.sum(value, axis=0, keepdims=True)
+    leave[-1].start()
     for copy in leave:
         copy.wait()
 
@@ -589,9 +620,9 @@
             pltpu.VMEM((2, edge_count), jnp.int32),
             pltpu.VMEM((edge_count,), f32),
             pltpu.VMEM((3, edge_count), f32),
-            pltpu.VMEM((24 * tiles, run), f32),
+            pltpu.VMEM((up(4 * tiles, 8), run), f32),
             pltpu.VMEM((8, edge_count), f32),
-            pltpu.VMEM((8, count), f32),
+            pltpu.VMEM((up(4 * tiles, 8), run), f32),
             pltpu.VMEM((4 * rows, depth), f32),
             pltpu.VMEM((3 * rows, depth), f32),
             pltpu.VMEM((rows, run), f32),
@@ -601,10 +632,6 @@
         scratch += [pltpu.VMEM((n * depth, 3 * run), bf16) for n in (3, 1, 1)]
         scratch += [
             pltpu.VMEM((19 * h, depth), f32),
-            pltpu.VMEM((3 * rows, depth), f32),
-            pltpu.VMEM((rows, count), f32),
-            pltpu.VMEM((2 * depth, count), bf16),
-            pltpu.VMEM((24, count), f32),
             pltpu.SemaphoreType.DMA((5,)),
             pltpu.SemaphoreType.DMA((6,)),
             pltpu.SemaphoreType.REGULAR((len(groups),)),
@@ -615,14 +642,20 @@
         def exchange(*refs):
             exchange_kernel(plan, nx, ny, *refs)
 
+        def finish(*refs):
+            finish_kernel(plan, *refs)
+
         held = pl.pallas_call(
             exchange,
             out_shape=(
                 jax.ShapeDtypeStruct((19 * wx * wy, depth), f32),
-                jax.ShapeDtypeStruct((3, count), f32),
+                jax.ShapeDtypeStruct((3 * rows, depth), f32),
+                jax.ShapeDtypeStruct((rows, count), f32),
+                jax.ShapeDtypeStruct((2 * depth, count), bf16),
+                jax.ShapeDtypeStruct((24, count), f32),
             ),
             in_specs=[far] * 6,
-            out_specs=(vmem,) * 2,
+            out_specs=(vmem,) * 5,
             scratch_shapes=scratch,
             compiler_params=pltpu.CompilerParams(
                 collective_id=0, has_side_effects=True, vmem_limit_bytes=24 * 1024 * 1024
@@ -642,14 +675,14 @@
             ]
         )
         fresh, sampled = pl.pallas_call(
-            finish_kernel,
+            finish,
             out_shape=(
                 jax.ShapeDtypeStruct((19 * wx * wy, depth), f32),
                 jax.ShapeDtypeStruct((3, count), f32),
             ),
-            in_specs=[vmem] * 2,
+            in_specs=[vmem] * 5,
             out_specs=(far, far),
-            scratch_shapes=[pltpu.SemaphoreType.DMA((2,))],
+            scratch_shapes=[pltpu.VMEM((3, count), f32), pltpu.SemaphoreType.DMA((pieces + 1,))],
             compiler_params=pltpu.CompilerParams(vmem_limit_bytes=24 * 1024 * 1024),
             name="finish",
         )(*held)

time: 12.2 us -> 11.7 us (0.959)
  Pallas kernels: 11.3 us -> 10.8 us
    pallas_call x1, Pallas kernels: 10.5 us -> 9.92 us  [per_device(): pl.pallas_call(exchange, out_shape=(jax.ShapeDtypeStruct((19 * wx * wy, d...]
where the time goes in v3:
time: 11.7 us; the launch traced here: 11.4 us
  Pallas kernels  10.8 us (92%)
  between operations  0.64 us (5%)
    pallas_call x1, Pallas kernels, per_device(): pl.pallas_call(exchange, out_shape=(jax.ShapeDtypeStruct((19 * wx * wy, d...  9.92 us
    pallas_call x1, Pallas kernels, per_device(): pl.pallas_call(finish, out_shape=(jax.ShapeDtypeStruct((19 * wx * wy, dep...  0.87 us

profile of v3, /device:TPU:0, one launch (start us, length us, event | category | flops | bytes accessed | tf_op | source)
XLA Modules:
  0.0 11.4 jit_solution(8752889312919509021)
XLA Ops:
  0.6 9.9 %exchange.1 = (f32[1216,128]{1,0:T(8,128)S(1)}, f32[480,128]{1,0:T(8,128)S(1)}, f32[160,512]{1,0:T(8,128)S(1)}, bf16[256,512]{1,0:T(8,128)(2,1)S(1)}, f32[24,512]{1,0:T(8,128)S(1)}) custom-call(f32[1216,128]{1,0:T(8,128)} %bitcast.2, s32[3,512]{1,0:T(4,128)} %refs_1_.1, f32[3,512]{1,0:T(4,128)} %refs_2_.1, s32[2,1536]{1,0:T(2,128)} %refs_3_.1, ...), custom_call_target="tpu_custom_call" | custom-call | tf_op jit(solution)/shard_map/exchange/pallas_call | solution.py:648
  10.6 0.9 %finish.1 = (f32[1216,128]{1,0:T(8,128)}, f32[3,512]{1,0:T(4,128)}) custom-call(f32[1216,128]{1,0:T(8,128)S(1)} %get-tuple-element.9.refs_0_, f32[480,128]{1,0:T(8,128)S(1)} %get-tuple-element.10.refs_1_, f32[160,512]{1,0:T(8,128)S(1)} %get-tuple-element.11.refs_2_, bf16[256,512]{1,0:T(8,128)(2,1)S(1)} %get-tuple-element.12.refs_3_, ...), custom_call_target="tpu_custom_call" | custom-call | tf_op jit(solution)/shard_map/finish/pallas_call | solution.py:677

commit v4 on v3

--- a/solution.py
+++ b/solution.py
@@ -158,22 +158,11 @@
     flat = jnp.concatenate([plane[pl.ds(a, n), :] for a, n in spans], axis=0)
     value = jnp.concatenate([vel[pl.ds(k * rows + a, n), :] for k in range(3) for a, n in spans], axis=0)
     v_high, v_low = split(value)
-    value = jnp.dot(
-        jnp.concatenate(
-            [
-                jnp.concatenate([v_high, v_high], axis=1),
-                jnp.concatenate([v_low, jnp.zeros(v_low.shape, bf16)], axis=1),
-            ],
-            axis=0,
-        ),
-        along[...],
-        preferred_element_type=f32,
-    )
+    value = jnp.dot(jnp.concatenate([v_high, v_low, v_high], axis=1), along[...], preferred_element_type=f32)
     size = flat.shape[0]
     out = []
     for k in range(3):
-        both = value[k * size : (k + 1) * size] + value[(k + 3) * size : (k + 4) * size]
-        both = both * flat
+        both = value[k * size : (k + 1) * size] * flat
         acc = both[0:8]
         for r in range(8, size, 8):
             acc = acc + both[r : r + 8]
@@ -191,7 +180,7 @@
     ones_y, ones_l, ones_r, edge_pops, sems, load_sems, ready = scratch[53:]
     depth = pops.shape[1]
     load_into = (pops.at[pl.ds(0, 19 * own), :], base, frac, edges, stiff, rest)
-    loads_in = [pltpu.make_async_copy(sources[n], load_into[n], load_sems.at[n]) for n in range(6)]
+    loads_in = [pltpu.make_async_copy(sources[n], load_into[n], load_sems.at[min(n, 1)]) for n in range(6)]
     for n in (3, 2, 1, 5, 4, 0):
         loads_in[n].start()
     count = base.shape[1]
@@ -294,20 +283,24 @@
         pull[pl.ds(k, 3), :] = rest[...]
     half_of = lax.broadcasted_iota(jnp.int32, (8, edge_count), 0) // 4
     mine = [group == 2 * p + half_of for p in range(pairs)]
-    diff = jnp.zeros((8, edge_count), f32)
-    for p in range(pairs):
-        table = pos[pl.ds(8 * p, 8), :]
-        gathered = []
-        for k in range(0, edge_count, run):
-            at = [jnp.broadcast_to(value[:, k : k + run], (8, run)) for value in (head, tail)]
-            gathered.append(
-                jnp.take_along_axis(table, at[0], axis=1) - jnp.take_along_axis(table, at[1], axis=1)
-            )
-        diff = jnp.where(mine[p], jnp.concatenate(gathered, axis=1), diff)
+    tables = [pos[pl.ds(8 * p, 8), :] for p in range(pairs)]
+    pieces_of = []
+    for k in range(0, edge_count, run):
+        cols = slice(k, k + run)
+        heads_at, tails_at = (jnp.broadcast_to(value[:, cols], (8, run)) for value in (head, tail))
+        piece = jnp.zeros((8, run), f32)
+        fronts = [jnp.take_along_axis(table, heads_at, axis=1) for table in tables]
+        backs = [jnp.take_along_axis(table, tails_at, axis=1) for table in tables]
+        for p in range(pairs):
+            piece = jnp.where(mine[p][:, cols], fronts[p] - backs[p], piece)
+        pieces_of.append(piece)
+    diff = jnp.concatenate(pieces_of, axis=1)
     stretch = stiff[...].reshape(1, edge_count) * (diff - pull[...])
     terms = jnp.concatenate([jnp.where(mine[p], stretch, 0.0) for p in range(pairs)], axis=0)
-    spot = lax.broadcasted_iota(jnp.int32, (run, edge_count), 0)
-    hot = jnp.where(spot == head, 1.0, jnp.where(spot == tail, -1.0, 0.0)).astype(bf16)
+    spot = lax.broadcasted_iota(jnp.int32, (run, edge_count), 0).astype(f32).astype(bf16)
+    one, none = jnp.ones((), bf16), jnp.zeros((), bf16)
+    heads, tails = (value.astype(f32).astype(bf16) for value in (head, tail))
+    hot = jnp.where(spot == heads, one, jnp.where(spot == tails, -one, none))
     part = 8 * pairs
     summed = transposed_dot(halves(terms), hot)
     mem[...] = -(summed[0:part] + summed[part : 2 * part])
@@ -425,6 +418,11 @@
         def _():
             force_copies[n].start()
 
+    gap = wrap(lax.broadcasted_iota(jnp.int32, (depth, count), 0) - (base[2:3, :] - 1), depth)
+    z_high, z_low = split(pick4(gap, [w[2:3] for w in weights]))
+    for k, value in enumerate((z_high, z_high, z_low)):
+        along[pl.ds(k * depth, depth), :] = value
+
     for i in (2, 3, 0, 1):
 
         @pl.when(led[i] > 0)
@@ -437,11 +435,6 @@
             def _():
                 force_copies[n].start()
                 macro_copies[n].start()
-
-    gap = wrap(lax.broadcasted_iota(jnp.int32, (depth, count), 0) - (base[2:3, :] - 1), depth)
-    z_high, z_low = split(pick4(gap, [w[2:3] for w in weights]))
-    along[pl.ds(0, depth), :] = z_high
-    along[pl.ds(depth, depth), :] = z_low
 
     comp_of = lane // (window * tiles)
     comps_of = jnp.concatenate([comp_of] * 3, axis=1)
@@ -564,8 +557,10 @@
             dst = [plan.there(c, sides[n]) - at for c in plan.force[n]]
             move(fr[n], list(range(plan.force_rows[n])), placed[n], dst)
         parts = jnp.concatenate([fr[order[0]][...], placed[order[1]][...], placed[order[2]][...]], axis=1)
-        parts = jnp.concatenate([jnp.where(comps_of == c, parts, 0.0) for c in range(3)], axis=0)
-        value = transposed_dot(halves(parts), ones[...])
+        rounded = parts.astype(bf16).astype(f32)
+        both = (rounded, parts - rounded)
+        parts = jnp.concatenate([jnp.where(comps_of == c, value, 0.0) for value in both for c in range(3)], axis=0)
+        value = transposed_dot(parts.astype(bf16), ones[...])
         for c in range(3):
             here = pl.ds(c * rows + at, 3 * h)
             both = value[3 * h * c : 3 * h * (c + 1)] + value[3 * h * (c + 3) : 3 * h * (c + 4)]
@@ -633,7 +628,7 @@
         scratch += [
             pltpu.VMEM((19 * h, depth), f32),
             pltpu.SemaphoreType.DMA((5,)),
-            pltpu.SemaphoreType.DMA((6,)),
+            pltpu.SemaphoreType.DMA((2,)),
             pltpu.SemaphoreType.REGULAR((len(groups),)),
         ]
         vmem = pl.BlockSpec(memory_space=pltpu.VMEM)
@@ -651,7 +646,7 @@
                 jax.ShapeDtypeStruct((19 * wx * wy, depth), f32),
                 jax.ShapeDtypeStruct((3 * rows, depth), f32),
                 jax.ShapeDtypeStruct((rows, count), f32),
-                jax.ShapeDtypeStruct((2 * depth, count), bf16),
+                jax.ShapeDtypeStruct((3 * depth, count), bf16),
                 jax.ShapeDtypeStruct((24, count), f32),
             ),
             in_specs=[far] * 6,

time: 11.7 us -> 11.6 us (level)
  no operation moved by 1% of the time
where the time goes in v4:
time: 11.6 us; the launch traced here: 11.4 us
  Pallas kernels  10.8 us (93%)
  between operations  0.64 us (6%)
    pallas_call x1, Pallas kernels, per_device(): pl.pallas_call(exchange, out_shape=(jax.ShapeDtypeStruct((19 * wx * wy, d...  9.88 us
    pallas_call x1, Pallas kernels, per_device(): pl.pallas_call(finish, out_shape=(jax.ShapeDtypeStruct((19 * wx * wy, dep...  0.87 us

profile of v4, /device:TPU:0, one launch (start us, length us, event | category | flops | bytes accessed | tf_op | source)
XLA Modules:
  0.0 11.4 jit_solution(7256038460360698334)
XLA Ops:
  0.6 9.9 %exchange.1 = (f32[1216,128]{1,0:T(8,128)S(1)}, f32[480,128]{1,0:T(8,128)S(1)}, f32[160,512]{1,0:T(8,128)S(1)}, bf16[384,512]{1,0:T(8,128)(2,1)S(1)}, f32[24,512]{1,0:T(8,128)S(1)}) custom-call(f32[1216,128]{1,0:T(8,128)} %bitcast.2, s32[3,512]{1,0:T(4,128)} %refs_1_.1, f32[3,512]{1,0:T(4,128)} %refs_2_.1, s32[2,1536]{1,0:T(2,128)} %refs_3_.1, ...), custom_call_target="tpu_custom_call" | custom-call | tf_op jit(solution)/shard_map/exchange/pallas_call | solution.py:643
  10.5 0.9 %finish.1 = (f32[1216,128]{1,0:T(8,128)}, f32[3,512]{1,0:T(4,128)}) custom-call(f32[1216,128]{1,0:T(8,128)S(1)} %get-tuple-element.9.refs_0_, f32[480,128]{1,0:T(8,128)S(1)} %get-tuple-element.10.refs_1_, f32[160,512]{1,0:T(8,128)S(1)} %get-tuple-element.11.refs_2_, bf16[384,512]{1,0:T(8,128)(2,1)S(1)} %get-tuple-element.12.refs_3_, ...), custom_call_target="tpu_custom_call" | custom-call | tf_op jit(solution)/shard_map/finish/pallas_call | solution.py:672

commit v5 on v4

--- a/solution.py
+++ b/solution.py
@@ -403,7 +403,7 @@
     for n in (4, 5):
         pack(n)
 
-    for n in (4, 5):
+    for n in (5, 4):
 
         @pl.when(lead[n] == 0)
         def _():
@@ -412,7 +412,7 @@
     spread([(left, right - left)])
     for n in (4, 5):
         move(comb, [plan.row(x, y) for x, y in plan.force[n]], fs[n], list(range(plan.force_rows[n])))
-    for n in (4, 5):
+    for n in (5, 4):
 
         @pl.when(lead[n] == 0)
         def _():

time: 11.6 us -> 11.6 us (level)
  no operation moved by 1% of the time
where the time goes in v5:
time: 11.6 us; the launch traced here: 11.4 us
  Pallas kernels  10.8 us (93%)
  between operations  0.64 us (6%)
    pallas_call x1, Pallas kernels, per_device(): pl.pallas_call(exchange, out_shape=(jax.ShapeDtypeStruct((19 * wx * wy, d...  9.88 us
    pallas_call x1, Pallas kernels, per_device(): pl.pallas_call(finish, out_shape=(jax.ShapeDtypeStruct((19 * wx * wy, dep...  0.87 us

profile of v5, /device:TPU:0, one launch (start us, length us, event | category | flops | bytes accessed | tf_op | source)
XLA Modules:
  0.0 11.4 jit_solution(8690555391988981776)
XLA Ops:
  0.6 9.9 %exchange.1 = (f32[1216,128]{1,0:T(8,128)S(1)}, f32[480,128]{1,0:T(8,128)S(1)}, f32[160,512]{1,0:T(8,128)S(1)}, bf16[384,512]{1,0:T(8,128)(2,1)S(1)}, f32[24,512]{1,0:T(8,128)S(1)}) custom-call(f32[1216,128]{1,0:T(8,128)} %bitcast.2, s32[3,512]{1,0:T(4,128)} %refs_1_.1, f32[3,512]{1,0:T(4,128)} %refs_2_.1, s32[2,1536]{1,0:T(2,128)} %refs_3_.1, ...), custom_call_target="tpu_custom_call" | custom-call | tf_op jit(solution)/shard_map/exchange/pallas_call | solution.py:643
  10.5 0.9 %finish.1 = (f32[1216,128]{1,0:T(8,128)}, f32[3,512]{1,0:T(4,128)}) custom-call(f32[1216,128]{1,0:T(8,128)S(1)} %get-tuple-element.9.refs_0_, f32[480,128]{1,0:T(8,128)S(1)} %get-tuple-element.10.refs_1_, f32[160,512]{1,0:T(8,128)S(1)} %get-tuple-element.11.refs_2_, bf16[384,512]{1,0:T(8,128)(2,1)S(1)} %get-tuple-element.12.refs_3_, ...), custom_call_target="tpu_custom_call" | custom-call | tf_op jit(solution)/shard_map/finish/pallas_call | solution.py:672
